TPU v7x, 32 devices: a 4x2x2 block of a 4x4x8 slice. The times are simulated.
32 devices in a mesh: dp: 4 (over y, z), ep: 8 (over x, core).
Axes of the slice: x: 4, y: 2, z: 2, core: 2. Of those that a mesh axis runs over, the one named last changes fastest.
The devices are a block of a 4x4x8 slice.
Arguments:
- h0: bfloat16 [32, 512, 2048], P(('dp', 'ep')), parts along dimension 0
- idx: int32 [32, 512, 6], P(('dp', 'ep')), parts along dimension 0
- slot: int32 [32, 512, 6], P(('dp', 'ep')), parts along dimension 0
- ln_attn: bfloat16 [2048], replicated
- wq: bfloat16 [2048, 2048], replicated
- wk: bfloat16 [2048, 2048], replicated
- wv: bfloat16 [2048, 2048], replicated
- wo: bfloat16 [2048, 2048], replicated
- ln_ffn: bfloat16 [2048], replicated
- ws1: bfloat16 [2048, 2816], replicated
- ws3: bfloat16 [2048, 2816], replicated
- ws2: bfloat16 [2816, 2048], replicated
- ln_moe: bfloat16 [2048], replicated
- wr: bfloat16 [2048, 64], replicated
- ue1: bfloat16 [64, 2048, 1408], P('ep')
- ue3: bfloat16 [64, 2048, 1408], P('ep')
- ue2: bfloat16 [64, 1408, 2048], P('ep')
Outputs:
- output: bfloat16 [32, 512, 2048], P(('dp', 'ep')), parts along dimension 0
There are 4 independent parts. A program takes and returns all parts, laid end to end along the dimension named above; an argument that names none is the same for every part.
All inputs are finite; a program needn't handle non-finite values.
Results may differ from a plain program's by a relative error of at most 0.0103379.
Values are sent between devices in bfloat16 or wider.
A program may use at most 768 MiB of HBM per device.

v0:
```python
import jax
import jax.numpy as jnp
from jax import lax
from jax.sharding import PartitionSpec as P

HEAD = 128
EPS = 1e-6
CAP_FACTOR = 2


def _mm(form, a, b):
    return jnp.einsum(form, a, b, preferred_element_type=jnp.float32)


def _rms(x, w):
    xf = x.astype(jnp.float32)
    r = lax.rsqrt(jnp.mean(xf * xf, axis=-1, keepdims=True) + EPS)
    return (xf * r * w.astype(jnp.float32)).astype(jnp.bfloat16)


def _rope(x):
    s, half = x.shape[1], x.shape[-1] // 2
    freq = 10000.0 ** (-jnp.arange(half, dtype=jnp.float32) / half)
    ang = jnp.arange(s, dtype=jnp.float32)[:, None] * freq[None, :]
    c = jnp.cos(ang)[None, :, None, :]
    sn = jnp.sin(ang)[None, :, None, :]
    x1, x2 = x[..., :half], x[..., half:]
    return jnp.concatenate([x1 * c - x2 * sn, x2 * c + x1 * sn], axis=-1)


def _dense(h0, ln_attn, wq, wk, wv, wo, ln_ffn, ws1, ws3, ws2):
    b, s, _ = h0.shape
    nh = wq.shape[1] // HEAD
    x1 = _rms(h0, ln_attn)
    q = _rope(_mm('bsd,de->bse', x1, wq).reshape(b, s, nh, HEAD)).astype(jnp.bfloat16)
    k = _rope(_mm('bsd,de->bse', x1, wk).reshape(b, s, nh, HEAD)).astype(jnp.bfloat16)
    v = _mm('bsd,de->bse', x1, wv).astype(jnp.bfloat16).reshape(b, s, nh, HEAD)
    sc = _mm('bqhe,bkhe->bhqk', q, k) * HEAD ** -0.5
    causal = jnp.arange(s)[:, None] >= jnp.arange(s)[None, :]
    p = jax.nn.softmax(jnp.where(causal, sc, -1e30), axis=-1).astype(jnp.bfloat16)
    o = _mm('bhqk,bkhe->bqhe', p, v).astype(jnp.bfloat16).reshape(b, s, nh * HEAD)
    a = (h0.astype(jnp.float32) + _mm('bse,ed->bsd', o, wo)).astype(jnp.bfloat16)
    x2 = _rms(a, ln_ffn)
    hs = (jax.nn.silu(_mm('bsd,df->bsf', x2, ws1)) * _mm('bsd,df->bsf', x2, ws3)).astype(jnp.bfloat16)
    return a, _mm('bsf,fd->bsd', hs, ws2)


def _experts(x, ue1, ue3, ue2):
    he = (jax.nn.silu(_mm('gecd,edf->egcf', x, ue1)) * _mm('gecd,edf->egcf', x, ue3)).astype(jnp.bfloat16)
    return _mm('egcf,efd->gecd', he, ue2).astype(jnp.bfloat16)


def _gate(u, wr, gi):
    lg = _mm('td,de->te', u, wr)
    hit = gi[..., None] == jnp.arange(wr.shape[1], dtype=gi.dtype)
    return jax.nn.softmax(jnp.sum(jnp.where(hit, lg[:, None, :], 0.0), axis=-1), axis=-1)


def _route(q, gate, n):
    hit = q[..., None] == jnp.arange(n, dtype=q.dtype)
    disp = jnp.any(hit, axis=-2).astype(jnp.bfloat16)
    comb = jnp.sum(jnp.where(hit, gate[..., None], 0.0), axis=-2)
    return disp, comb


def _parts(c):
    hi = c.astype(jnp.bfloat16)
    r = c - hi.astype(jnp.float32)
    mid = r.astype(jnp.bfloat16)
    lo = (r - mid.astype(jnp.float32)).astype(jnp.bfloat16)
    return hi, mid, lo


def solution(mesh):
    g_ = mesh.shape['ep']
    rows = P(('dp', 'ep'))
    rep = P()

    def local(h0, idx, slot, ln_attn, wq, wk, wv, wo, ln_ffn, ws1, ws3, ws2, ln_moe, wr, ue1, ue3, ue2):
        b, s, d = h0.shape
        top = idx.shape[-1]
        el = ue1.shape[0]
        ne = el * g_
        t = b * s
        cap = CAP_FACTOR * t * top // ne
        a, fo = _dense(h0, ln_attn, wq, wk, wv, wo, ln_ffn, ws1, ws3, ws2)
        u = _rms(h0, ln_moe).reshape(t, d)
        gi = idx.reshape(t, top)
        sl = slot.reshape(t, top)
        gate = _gate(u, wr, gi)
        disp, comb = _route(gi * cap + sl, gate, ne * cap)
        send = _mm('tr,td->rd', disp, u).astype(jnp.bfloat16).reshape(g_, el, cap, d)
        recv = lax.all_to_all(send, 'ep', 0, 0, tiled=True)
        y = _experts(recv, ue1, ue3, ue2)
        back = lax.all_to_all(y, 'ep', 0, 0, tiled=True).reshape(ne * cap, d)
        m = sum(_mm('tr,rd->td', p, back) for p in _parts(comb))
        out = a.astype(jnp.float32) + fo + m.reshape(b, s, d)
        return out.astype(jnp.bfloat16)

    specs = (rows, rows, rows) + (rep,) * 11 + (P('ep'), P('ep'), P('ep'))
    return jax.shard_map(local, mesh=mesh, in_specs=specs, out_specs=rows, check_vma=False)
```

profile of v0, /device:TPU:81, one launch (start us, length us, event | category | flops | bytes accessed | tf_op | source)
XLA Modules:
  0.0 883.7 jit_solution(2415741048852610195)
XLA Ops:
  0.0 0.0 copy-start
  0.0 0.0 copy-start.7
  0.0 2.1 fusion.29
  2.1 0.0 copy-start.10
  2.2 0.7 bitcast_add_fusion
  2.9 0.0 copy-start.2
  2.9 11.1 %fusion.1 = pred[512,6144]{1,0:T(8,128)(4,1)S(1)} fusion(s32[512,6]{0,1:T(8,128)S(1)} %bitcast_add_fusion), kind=kLoop, calls=%fused_computation.3 | loop fusion | flops 34603008 | bytes 3158016 | tf_op jit(solution)/shard_map/reduce_or | solution.py:61
  14.0 0.0 copy-done.7
  14.0 0.0 copy-start.5
  14.1 19.0 %convolution_convert_fusion = bf16[6144,2048]{1,0:T(8,128)(2,1)} fusion(pred[512,6144]{1,0:T(8,128)(4,1)S(1)} %fusion.1, bf16[1,512,2048]{2,1,0:T(8,128)(2,1)} %param.17, f32[2048]{0:T(1024)S(1)} %convert_element_type.103, f32[512]{0:T(512)S(1)} %add_rsqrt_fusion.1), kind=kOutput, calls=%fused_computation.12 | convolution fusion | flops 12901679104 | bytes 30418944 | tf_op jit(solution)/shard_map/tr,td->rd/dot_general | solution.py:12
  33.0 0.0 copy-done.10
  33.0 0.0 copy-done.2
  33.0 0.0 copy-done.5
  33.0 284.8 %all_to_all.10 = bf16[8,8,96,2048]{3,2,1,0:T(8,128)(2,1)} all-to-all(bf16[8,8,96,2048]{3,2,1,0:T(8,128)(2,1)} %bitcast.98), channel_id=1, replica_groups=mesh['dp'=4,'ep'=8] {'ep'}, dimensions={0} | all-to-all | bytes 50331648 | tf_op jit(solution)/shard_map/all_to_all | solution.py:93
  317.8 49.0 %fusion.4 = f32[8,8,96,1408]{3,2,1,0:T(8,128)} fusion(bf16[8,2048,1408]{2,1,0:T(8,128)(2,1)} %param.32, bf16[8,8,96,2048]{3,2,1,0:T(8,128)(2,1)} %all_to_all.10), kind=kOutput, calls=%fused_computation.6 | convolution fusion | flops 35433480192 | bytes 105906176 | tf_op jit(solution)/shard_map/gecd,edf->egcf/dot_general | solution.py:12
  366.9 58.6 %multiply_convert_fusion = bf16[8,8,96,1408]{3,2,1,0:T(8,128)(2,1)} fusion(f32[8,8,96,1408]{3,2,1,0:T(8,128)} %fusion.4, bf16[8,2048,1408]{2,1,0:T(8,128)(2,1)} %param.31, bf16[8,8,96,2048]{3,2,1,0:T(8,128)(2,1)} %all_to_all.10), kind=kOutput, calls=%fused_computation.10 | convolution fusion | flops 35485384704 | bytes 123207680 | tf_op jit(solution)/shard_map/gecd,edf->egcf/dot_general | solution.py:12
  425.5 48.0 %convert_bitcast_fusion = bf16[8,8,96,2048]{3,2,0,1:T(8,128)(2,1)} fusion(bf16[8,8,96,1408]{3,2,1,0:T(8,128)(2,1)} %multiply_convert_fusion, bf16[8,1408,2048]{2,1,0:T(8,128)(2,1)} %param.33), kind=kOutput, calls=%fused_computation.11 | convolution fusion | flops 35446063104 | bytes 88604672 | tf_op jit(solution)/shard_map/egcf,efd->gecd/dot_general | solution.py:12
  473.5 21.0 %copy.59 = bf16[8,8,96,2048]{3,2,1,0:T(8,128)(2,1)} copy(bf16[8,8,96,2048]{3,2,0,1:T(8,128)(2,1)} %convert_bitcast_fusion) | data formatting | bytes 50331648 | tf_op jit(solution)/shard_map/convert_element_type | solution.py:50
  494.6 0.0 copy-start.4
  494.6 0.0 copy-start.8
  494.6 0.0 copy-start.1
  494.6 0.0 copy-start.11
  494.6 7.5 all-to-all-start.1
  502.1 0.0 copy-done.4
  502.1 0.0 copy-done.8
  502.1 0.0 copy-done.1
  502.1 0.0 copy-done.11
  502.1 9.2 %convolution_convert_fusion.1 = bf16[512,2048]{1,0:T(8,128)(2,1)} fusion(bf16[2048,2048]{1,0:T(8,128)(2,1)} %param.23, bf16[1,512,2048]{2,1,0:T(8,128)(2,1)S(1)} %copy-done.1, f32[2048]{0:T(1024)S(1)} %convert_element_type.91, f32[512]{0:T(512)S(1)} %copy-done.11), kind=kOutput, calls=%fused_computation.48 | convolution fusion | flops 4300210176 | bytes 12593152 | tf_op jit(solution)/shard_map/bsd,de->bse/dot_general | solution.py:12
  511.3 3.9 copy.66
  515.3 12.3 %copy.68 = bf16[2048,2048]{1,0:T(8,128)(2,1)} copy(bf16[2048,2048]{0,1:T(8,128)(2,1)} %bitcast.99) | data formatting | bytes 16777216 | tf_op jit(solution)/shard_map/bsd,de->bse/dot_general | solution.py:12
  527.6 0.0 copy-start.9
  527.6 0.0 copy-start.6
  527.6 12.3 %copy.67 = bf16[2048,2048]{1,0:T(8,128)(2,1)} copy(bf16[2048,2048]{0,1:T(8,128)(2,1)} %bitcast.100) | data formatting | bytes 16777216 | tf_op jit(solution)/shard_map/bsd,de->bse/dot_general | solution.py:12
  539.9 0.0 copy-done.9
  539.9 0.0 copy-done
  539.9 0.0 copy-done.6
  539.9 0.8 fusion.57
  540.7 0.1 select_reduce_fusion.1
  540.9 0.0 slice-start
  540.9 0.1 iota_compare_fusion.1
  541.0 0.5 fusion.60
  541.5 0.0 slice-start.1
  541.6 7.8 convolution_bitcast_fusion
  549.4 0.0 slice-done
  549.4 0.0 slice-done.1
  549.4 4.7 convolution_bitcast_fusion.1
  554.1 1.5 fusion.51
  555.7 8.2 fusion.38
  563.9 17.3 %fusion.69 = (f32[16,512]{1,0:T(8,128)S(1)}, f32[16,512,512]{1,2,0:T(8,128)}) fusion(f32[16,512,512]{1,2,0:T(8,128)} %fusion.38, pred[512,512]{0,1:T(8,128)(4,1)S(1)} %iota_compare_fusion.1), kind=kOutput, calls=%fused_computation.91 | output fusion | flops 25166336 | bytes 33849344 | tf_op jit(solution)/shard_map/sub | solution.py:40
  581.2 7.7 fusion.48
  588.9 8.4 fusion.31
  597.3 0.0 copy-start.12
  597.4 1.3 copy-done.12
  598.6 0.0 copy-start.3
  598.6 11.2 %fusion.54 = f32[512,2816]{1,0:T(8,128)} fusion(bf16[2048,2816]{1,0:T(8,128)(2,1)} %param.26, bf16[1,512,2048]{2,1,0:T(8,128)(2,1)S(1)} %get-tuple-element.16, f32[2048]{0:T(1024)S(1)} %convert_element_type.100, f32[512]{0:T(512)S(1)} %add_rsqrt_fusion), kind=kOutput, calls=%fused_computation.75 | convolution fusion | flops 5909774336 | bytes 19408896 | tf_op jit(solution)/shard_map/bsd,df->bsf/dot_general | solution.py:12
  609.8 0.0 copy-done.3
  609.8 18.1 %select_reduce_fusion = f32[512,6144]{1,0:T(8,128)} fusion(f32[512,6]{0,1:T(8,128)S(1)} %fusion.61, s32[512,6]{0,1:T(8,128)S(1)} %copy-done.3), kind=kLoop, calls=%fused_computation.1 | loop fusion | flops 53477376 | bytes 12607488 | tf_op jit(solution)/shard_map/reduce_sum | solution.py:62
  627.9 147.5 %all-to-all-done.1 = bf16[8,8,96,2048]{3,2,1,0:T(8,128)(2,1)} async-done(((bf16[8,8,96,2048]{3,2,1,0:T(8,128)(2,1)}), bf16[8,8,96,2048]{3,2,1,0:T(8,128)(2,1)}, u32[]{:S(2)}, u32[]{:S(2)}) %all-to-all-start.1) | async-done | bytes 25165856 | tf_op jit(solution)/shard_map/all_to_all | solution.py:95
  775.5 30.1 %fusion.24 = f32[512,2048]{1,0:T(8,128)} fusion(bf16[6144,2048]{1,0:T(8,128)(2,1)} %bitcast.28, f32[512,6144]{1,0:T(8,128)} %select_reduce_fusion), kind=kOutput, calls=%fused_computation.29 | convolution fusion | flops 12906921984 | bytes 41943040 | tf_op jit(solution)/shard_map/tr,rd->td/dot_general | solution.py:12
  805.6 22.8 %fusion.16 = f32[512,2048]{1,0:T(8,128)} fusion(bf16[6144,2048]{1,0:T(8,128)(2,1)} %bitcast.28, f32[512,6144]{1,0:T(8,128)} %select_reduce_fusion), kind=kOutput, calls=%fused_computation.22 | convolution fusion | flops 12888047616 | bytes 41943040 | tf_op jit(solution)/shard_map/tr,rd->td/dot_general | solution.py:12
  828.4 0.0 copy-start.13
  828.4 30.2 %fusion.18 = f32[512,2048]{1,0:T(8,128)} fusion(bf16[6144,2048]{1,0:T(8,128)(2,1)} %bitcast.28, f32[512,6144]{1,0:T(8,128)} %select_reduce_fusion), kind=kOutput, calls=%fused_computation.24 | convolution fusion | flops 12897484800 | bytes 41943040 | tf_op jit(solution)/shard_map/tr,rd->td/dot_general | solution.py:12
  858.6 0.0 copy-done.13
  858.6 24.8 %fusion.35 = bf16[1,512,2048]{2,1,0:T(8,128)(2,1)} fusion(bf16[1,512,2048]{2,1,0:T(8,128)(2,1)S(1)} %copy-done.13, f32[512,2048]{1,0:T(8,128)} %fusion.24, f32[512,2048]{1,0:T(8,128)} %fusion.16, f32[512,2048]{1,0:T(8,128)} %fusion.18, bf16[2816,2048]{1,0:T(8,128)(2,1)} %param.28, f32[512,2816]{1,0:T(8,128)} %fusion.54, bf16[2048,2816]{1,0:T(8,128)(2,1)} %param.27, ...), kind=kOutput, calls=%fused_computation.47 | convolution fusion | flops 11830296576 | bytes 45623296 | tf_op jit(solution)/shard_map/bsf,fd->bsd/dot_general | solution.py:12
  (11 shorter events, 0.1 us)
Async XLA Ops:
  0.0 539.9 %copy-start = (bf16[2048,64]{0,1:T(8,128)(2,1)S(1)}, bf16[2048,64]{0,1:T(8,128)(2,1)}, u32[]{:S(2)}) copy-start(bf16[2048,64]{0,1:T(8,128)(2,1)} %param.30) | copy-start | bytes 786436
  0.0 14.0 %copy-start.7 = (bf16[2048]{0:T(1024)(128)(2,1)S(1)}, bf16[2048]{0:T(1024)(128)(2,1)}, u32[]{:S(2)}) copy-start(bf16[2048]{0:T(1024)(128)(2,1)} %param.29) | copy-start | bytes 12292
  2.1 30.9 %copy-start.10 = (f32[512]{0:T(512)}, f32[512]{0:T(512)S(1)}, u32[]{:S(2)}) copy-start(f32[512]{0:T(512)S(1)} %add_rsqrt_fusion.1) | copy-start | bytes 6148
  2.9 30.1 %copy-start.2 = (s32[512,6]{0,1:T(8,128)}, s32[512,6]{0,1:T(8,128)S(1)}, u32[]{:S(2)}) copy-start(s32[512,6]{0,1:T(8,128)S(1)} %bitcast_add_fusion) | copy-start | bytes 36868
  14.0 19.0 %copy-start.5 = (f32[2048]{0:T(1024)}, f32[2048]{0:T(1024)S(1)}, u32[]{:S(2)}) copy-start(f32[2048]{0:T(1024)S(1)} %convert_element_type.103) | copy-start | bytes 24580
  494.6 7.5 copy-start.4
  494.6 7.5 copy-start.8
  494.6 7.5 copy-start.1
  494.6 7.6 copy-start.11
  494.6 280.9 %all-to-all-start.1 = ((bf16[8,8,96,2048]{3,2,1,0:T(8,128)(2,1)}), bf16[8,8,96,2048]{3,2,1,0:T(8,128)(2,1)}, u32[]{:S(2)}, u32[]{:S(2)}) async-start(bf16[8,8,96,2048]{3,2,1,0:T(8,128)(2,1)} %copy.59), calls=%async_computation.1 | async-start | bytes 50331648 | tf_op jit(solution)/shard_map/all_to_all | solution.py:95
  527.6 12.3 %copy-start.9 = (bf16[2048]{0:T(1024)(128)(2,1)S(1)}, bf16[2048]{0:T(1024)(128)(2,1)}, u32[]{:S(2)}) copy-start(bf16[2048]{0:T(1024)(128)(2,1)} %param.25) | copy-start | bytes 12292
  527.6 12.3 %copy-start.6 = (f32[2048]{0:T(1024)S(1)}, f32[2048]{0:T(1024)}, u32[]{:S(2)}) copy-start(f32[2048]{0:T(1024)} %copy-done.5) | copy-start | bytes 24580
  540.9 8.5 slice-start
  541.5 7.9 slice-start.1
  597.3 1.3 copy-start.12
  598.6 11.2 %copy-start.3 = (s32[512,6]{0,1:T(8,128)S(1)}, s32[512,6]{0,1:T(8,128)}, u32[]{:S(2)}) copy-start(s32[512,6]{0,1:T(8,128)} %copy-done.2) | copy-start | bytes 36868
  828.4 30.2 %copy-start.13 = (bf16[1,512,2048]{2,1,0:T(8,128)(2,1)S(1)}, bf16[1,512,2048]{2,1,0:T(8,128)(2,1)}, u32[]{:S(2)}) copy-start(bf16[1,512,2048]{2,1,0:T(8,128)(2,1)} %copy-done.12) | copy-start | bytes 6291460
where the time goes:
time: 891 us; the launch traced here: 884 us
  matrix products  341 us (38%)
  blocking collectives  285 us (32%)
  waiting for transfers between devices  148 us (17%)
  other arithmetic  51.8 us (6%)
  local copies, waits for them, and re-layouts  50.9 us (6%)
    dot_general x16, matrix products, _mm(): return jnp.einsum(form, a, b, preferred_element_type=jnp.float32)  341 us
    all_to_all x1, blocking collectives, local(): recv = lax.all_to_all(send, 'ep', 0, 0, tiled=True)  285 us
    all_to_all x1, waiting for transfers between devices, local(): back = lax.all_to_all(y, 'ep', 0, 0, tiled=True).reshape(ne * cap, d)  148 us
    dot_general x2, local copies, waits for them, and re-layouts, _mm(): return jnp.einsum(form, a, b, preferred_element_type=jnp.float32)  24.6 us
    convert_element_type x1, local copies, waits for them, and re-layouts, _experts(): return _mm('egcf,efd->gecd', he, ue2).astype(jnp.bfloat16)  21 us
    reduce_sum x1, other arithmetic, _route(): comb = jnp.sum(jnp.where(hit, gate[..., None], 0.0), axis=-2)  18.1 us
  transfers between devices with their start and end apart: 1, of which 1 were waited for; matrix products, arithmetic and copies ran while one was open for 14% of the time, Pallas kernels for 0%

commit v1 on v0

--- a/solution.py
+++ b/solution.py
@@ -1,6 +1,8 @@
 import jax
 import jax.numpy as jnp
 from jax import lax
+from jax.experimental import pallas as pl
+from jax.experimental.pallas import tpu as pltpu
 from jax.sharding import PartitionSpec as P
 
 HEAD = 128
@@ -45,30 +47,316 @@
     return a, _mm('bsf,fd->bsd', hs, ws2)
 
 
-def _experts(x, ue1, ue3, ue2):
-    he = (jax.nn.silu(_mm('gecd,edf->egcf', x, ue1)) * _mm('gecd,edf->egcf', x, ue3)).astype(jnp.bfloat16)
-    return _mm('egcf,efd->gecd', he, ue2).astype(jnp.bfloat16)
-
-
-def _gate(u, wr, gi):
-    lg = _mm('td,de->te', u, wr)
-    hit = gi[..., None] == jnp.arange(wr.shape[1], dtype=gi.dtype)
-    return jax.nn.softmax(jnp.sum(jnp.where(hit, lg[:, None, :], 0.0), axis=-1), axis=-1)
-
-
-def _route(q, gate, n):
-    hit = q[..., None] == jnp.arange(n, dtype=q.dtype)
-    disp = jnp.any(hit, axis=-2).astype(jnp.bfloat16)
-    comb = jnp.sum(jnp.where(hit, gate[..., None], 0.0), axis=-2)
-    return disp, comb
-
-
-def _parts(c):
-    hi = c.astype(jnp.bfloat16)
-    r = c - hi.astype(jnp.float32)
-    mid = r.astype(jnp.bfloat16)
-    lo = (r - mid.astype(jnp.float32)).astype(jnp.bfloat16)
-    return hi, mid, lo
+VMEM_LIMIT = 66_000_000
+LANES = 128
+COLS = 256
+MESH = pl.DeviceIdType.MESH
+
+
+def _dispatch_kernel(el, cap, top, base_ref, ug_ref, wr_ref, x_ref, hit_ref, gr_ref):
+    t = hit_ref.shape[-1]
+    ne = wr_ref.shape[-1]
+    meta = ug_ref[0, t:t + 16, :t].astype(jnp.float32)
+    idx = meta[0:top].astype(jnp.int32)
+    row = idx * cap + meta[8:8 + top].astype(jnp.int32) - base_ref[0]
+    lg = lax.dot_general(wr_ref[...], ug_ref[0, :t, :], (((0,), (1,)), ((), ())), preferred_element_type=jnp.float32)
+    expert = lax.broadcasted_iota(jnp.int32, (ne, t), 0)
+    picked = [jnp.sum(jnp.where(expert == idx[j:j + 1], lg, 0.0), axis=0, keepdims=True) for j in range(top)]
+    high = picked[0]
+    for p in picked[1:]:
+        high = jnp.maximum(high, p)
+    ex = [jnp.exp(p - high) for p in picked]
+    den = ex[0]
+    for e in ex[1:]:
+        den = den + e
+    gate = [e / den for e in ex]
+    for e in range(el):
+        at = lax.broadcasted_iota(jnp.int32, (cap, t), 0) + e * cap
+        hit = jnp.zeros((cap, t), jnp.float32)
+        g = jnp.zeros((cap, t), jnp.float32)
+        for j in range(top):
+            same = at == row[j:j + 1]
+            hit = jnp.where(same, 1.0, hit)
+            g = jnp.where(same, gate[j], g)
+        hit_ref[0, e * cap:(e + 1) * cap, :] = hit.astype(jnp.bfloat16)
+        gr_ref[0, e * cap:(e + 1) * cap, :] = jnp.broadcast_to(jnp.sum(g, axis=1, keepdims=True), (cap, LANES))
+    half = el // 2
+
+    def column(c, _):
+        cols = pl.ds(pl.multiple_of(c * COLS, COLS), COLS)
+        x = jnp.dot(hit_ref[0], ug_ref[0, :t, cols], preferred_element_type=jnp.float32)
+        x_ref[:, 0, :, cols] = x.astype(jnp.bfloat16).reshape(el, cap, COLS)
+        return 0
+
+    lax.fori_loop(0, x_ref.shape[-1] // COLS, column, 0)
+
+
+def _dispatch(base, ug, wr, el, cap, top):
+    g, rows, d = ug.shape
+    t = rows - 16
+    n = el * cap
+    return pl.pallas_call(
+        lambda *refs: _dispatch_kernel(el, cap, top, *refs),
+        grid=(g,),
+        in_specs=[
+            pl.BlockSpec(memory_space=pltpu.SMEM),
+            pl.BlockSpec((1, rows, d), lambda i: (i, 0, 0)),
+            pl.BlockSpec(wr.shape, lambda i: (0, 0)),
+        ],
+        out_specs=[
+            pl.BlockSpec((el, 1, cap, d), lambda i: (0, i, 0, 0)),
+            pl.BlockSpec((1, n, t), lambda i: (i, 0, 0)),
+            pl.BlockSpec((1, n, LANES), lambda i: (i, 0, 0)),
+        ],
+        out_shape=[
+            jax.ShapeDtypeStruct((el, g, cap, d), jnp.bfloat16),
+            jax.ShapeDtypeStruct((g, n, t), jnp.bfloat16),
+            jax.ShapeDtypeStruct((g, n, LANES), jnp.float32),
+        ],
+        compiler_params=pltpu.CompilerParams(vmem_limit_bytes=VMEM_LIMIT),
+        cost_estimate=pl.CostEstimate(flops=2 * g * n * t * d, bytes_accessed=60_000_000, transcendentals=0),
+        name='dispatch',
+    )(base, ug, wr)
+
+
+def _up_kernel(x_ref, w1_ref, w3_ref, h_ref):
+    def column(c, _):
+        cols = pl.ds(pl.multiple_of(c * LANES, LANES), LANES)
+        w = jnp.concatenate([w1_ref[0, :, cols], w3_ref[0, :, cols]], axis=1)
+        r = jnp.dot(x_ref[0], w, preferred_element_type=jnp.float32)
+        h_ref[0, :, cols] = (jax.nn.silu(r[:, :LANES]) * r[:, LANES:]).astype(jnp.bfloat16)
+        return 0
+
+    lax.fori_loop(0, h_ref.shape[-1] // LANES, column, 0)
+
+
+def _up(x, ue1, ue3):
+    el, n, d = x.shape
+    f = ue1.shape[-1]
+    return pl.pallas_call(
+        _up_kernel,
+        grid=(el,),
+        in_specs=[
+            pl.BlockSpec((1, n, d), lambda i: (i, 0, 0)),
+            pl.BlockSpec((1, d, f), lambda i: (i, 0, 0)),
+            pl.BlockSpec((1, d, f), lambda i: (i, 0, 0)),
+        ],
+        out_specs=pl.BlockSpec((1, n, f), lambda i: (i, 0, 0)),
+        out_shape=jax.ShapeDtypeStruct((el, n, f), jnp.bfloat16),
+        compiler_params=pltpu.CompilerParams(vmem_limit_bytes=VMEM_LIMIT),
+        cost_estimate=pl.CostEstimate(flops=4 * el * n * f * d, bytes_accessed=100_000_000, transcendentals=0),
+        name='up',
+    )(x, ue1, ue3)
+
+
+def _down_kernel(nc, g, he_hbm, w_hbm, hit_hbm, gr_hbm, out_ref,
+                 he, w, hit, gr, y, p, ra, rb, rf,
+                 he_sem, w_sem, in_sem, a_send, a_recv, b_send, b_recv, f_send, f_recv, a_free, b_free, f_free):
+    el, n, f = he.shape
+    t = hit.shape[-1]
+    cap = n // g
+    chips = g // 2
+    me = lax.axis_index('ep')
+    core, chip = lax.rem(me, 2), lax.div(me, 2)
+    lchip, rchip, ochip = lax.rem(chip + chips - 1, chips), lax.rem(chip + 1, chips), lax.rem(chip + 2, chips)
+    mate, left, right = me + 1 - 2 * core, 2 * lchip + core, 2 * rchip + core
+
+    def he_copy(e):
+        return pltpu.make_async_copy(he_hbm.at[e], he.at[e], he_sem.at[e])
+
+    def w_copy(q):
+        e, c, slot = lax.rem(q, el), lax.div(q, el), lax.rem(q, 4)
+        cols = pl.ds(pl.multiple_of(c * COLS, COLS), COLS)
+        return pltpu.make_async_copy(w_hbm.at[e, :, cols], w.at[slot], w_sem.at[slot])
+
+    hit_copy = pltpu.make_async_copy(hit_hbm, hit, in_sem.at[0])
+    gr_copy = pltpu.make_async_copy(gr_hbm, gr, in_sem.at[1])
+
+    def a_copy(c):
+        return pltpu.make_async_remote_copy(
+            src_ref=p.at[lax.rem(c, 3), 1 - core], dst_ref=ra.at[lax.rem(c, 2)],
+            send_sem=a_send.at[lax.rem(c, 2)], recv_sem=a_recv.at[lax.rem(c, 2)],
+            device_id={'ep': mate}, device_id_type=MESH)
+
+    def b_copy(c, way):
+        return pltpu.make_async_remote_copy(
+            src_ref=p.at[lax.rem(c, 3), core, ochip, :, pl.ds(way * LANES, LANES)], dst_ref=rb.at[lax.rem(c, 2), way],
+            send_sem=b_send.at[lax.rem(c, 3), way], recv_sem=b_recv.at[lax.rem(c, 2), way],
+            device_id={'ep': (left, right)[way]}, device_id_type=MESH)
+
+    def f_copy(c, way):
+        return pltpu.make_async_remote_copy(
+            src_ref=p.at[lax.rem(c, 3), core, (lchip, rchip)[way]], dst_ref=rf.at[lax.rem(c, 2), way],
+            send_sem=f_send.at[lax.rem(c, 3), way], recv_sem=f_recv.at[lax.rem(c, 2), way],
+            device_id={'ep': (left, right)[way]}, device_id_type=MESH)
+
+    def signal(sem, dev):
+        pl.semaphore_signal(sem, inc=1, device_id={'ep': dev}, device_id_type=MESH)
+
+    w_copy(0).start()
+    for e in range(el):
+        he_copy(e).start()
+        if e < 2:
+            w_copy(e + 1).start()
+    hit_copy.start()
+    gr_copy.start()
+
+    barrier = pltpu.get_barrier_semaphore()
+    for dev in (mate, left, right):
+        signal(barrier, dev)
+    pl.semaphore_wait(barrier, 3)
+
+    def chunk(i, _):
+        @pl.when(i < nc)
+        def _():
+            def expert(e, _):
+                q = i * el + e
+
+                @pl.when(q + 3 < nc * el)
+                def _():
+                    w_copy(q + 3).start()
+
+                @pl.when(i == 0)
+                def _():
+                    he_copy(e).wait()
+
+                w_copy(q).wait()
+                yy = jnp.dot(he[e], w[lax.rem(q, 4)], preferred_element_type=jnp.float32)
+                y[:, e] = yy.astype(jnp.bfloat16).reshape(g, cap, COLS)
+                return 0
+
+            lax.fori_loop(0, el, expert, 0)
+
+        @pl.when(jnp.logical_and(i >= 1, i <= nc))
+        def _():
+            c = i - 1
+            slot = lax.rem(c, 3)
+            cc = a_copy(c)
+            cc.wait_recv()
+            cc.wait_send()
+            p[slot, core] += ra[lax.rem(c, 2)]
+
+            @pl.when(c < nc - 2)
+            def _():
+                signal(a_free, mate)
+
+            @pl.when(c >= 2)
+            def _():
+                pl.semaphore_wait(b_free.at[0], 1)
+                pl.semaphore_wait(b_free.at[1], 1)
+
+            b_copy(c, 0).start()
+            b_copy(c, 1).start()
+
+        @pl.when(jnp.logical_and(i >= 2, i <= nc + 1))
+        def _():
+            c = i - 2
+            slot = lax.rem(c, 3)
+            b_copy(c, 0).wait_recv()
+            b_copy(c, 1).wait_recv()
+            p[slot, core, lchip, :, :LANES] += rb[lax.rem(c, 2), 0]
+            p[slot, core, rchip, :, LANES:] += rb[lax.rem(c, 2), 1]
+
+            @pl.when(c < nc - 2)
+            def _():
+                signal(b_free.at[0], right)
+                signal(b_free.at[1], left)
+
+            @pl.when(c >= 2)
+            def _():
+                pl.semaphore_wait(f_free.at[0], 1)
+                pl.semaphore_wait(f_free.at[1], 1)
+
+            f_copy(c, 0).start()
+            f_copy(c, 1).start()
+
+        @pl.when(i >= 3)
+        def _():
+            c = i - 3
+            f_copy(c, 0).wait_recv()
+            f_copy(c, 1).wait_recv()
+            cols = pl.ds(pl.multiple_of(c * COLS, COLS), COLS)
+            out_ref[:, cols] = p[lax.rem(c, 3), core, chip] + (rf[lax.rem(c, 2), 0] + rf[lax.rem(c, 2), 1])
+
+            @pl.when(c < nc - 2)
+            def _():
+                signal(f_free.at[0], right)
+                signal(f_free.at[1], left)
+
+            for way in range(2):
+                b_copy(c, way).wait_send()
+                f_copy(c, way).wait_send()
+
+        @pl.when(i < nc)
+        def _():
+            @pl.when(i == 0)
+            def _():
+                hit_copy.wait()
+                gr_copy.wait()
+
+            slot = lax.rem(i, 3)
+
+            def combine(kk):
+                def dest(dc, _):
+                    dd = 2 * dc + kk
+                    scale = gr[dd]
+                    z = y[dd].reshape(n, COLS).astype(jnp.float32) * jnp.concatenate([scale, scale], axis=1)
+                    hi = z.astype(jnp.bfloat16)
+                    z = z - hi.astype(jnp.float32)
+                    mid = z.astype(jnp.bfloat16)
+                    lo = (z - mid.astype(jnp.float32)).astype(jnp.bfloat16)
+                    r = lax.dot_general(hit[dd], jnp.concatenate([hi, mid, lo], axis=1), (((0,), (0,)), ((), ())),
+                                        preferred_element_type=jnp.float32)
+                    p[slot, kk, dc] = r[:, :COLS] + (r[:, COLS:2 * COLS] + r[:, 2 * COLS:])
+                    return 0
+
+                lax.fori_loop(0, chips, dest, 0)
+
+            combine(1 - core)
+
+            @pl.when(i >= 2)
+            def _():
+                pl.semaphore_wait(a_free, 1)
+
+            a_copy(i).start()
+            combine(core)
+
+        return 0
+
+    lax.fori_loop(0, nc + 3, chunk, 0)
+
+
+def _down(he, ue2, hit, gr, g):
+    el, n, f = he.shape
+    d = ue2.shape[-1]
+    t = hit.shape[-1]
+    nc = d // COLS
+    chips = g // 2
+    dma = pltpu.SemaphoreType.DMA
+    reg = pltpu.SemaphoreType.REGULAR
+    return pl.pallas_call(
+        lambda *refs: _down_kernel(nc, g, *refs),
+        in_specs=[pl.BlockSpec(memory_space=pl.ANY)] * 4,
+        out_specs=pl.BlockSpec(memory_space=pltpu.VMEM),
+        out_shape=jax.ShapeDtypeStruct((t, d), jnp.float32),
+        scratch_shapes=[
+            pltpu.VMEM((el, n, f), jnp.bfloat16),
+            pltpu.VMEM((4, f, COLS), jnp.bfloat16),
+            pltpu.VMEM(hit.shape, jnp.bfloat16),
+            pltpu.VMEM(gr.shape, jnp.float32),
+            pltpu.VMEM((g, el, n // g, COLS), jnp.bfloat16),
+            pltpu.VMEM((3, 2, chips, t, COLS), jnp.float32),
+            pltpu.VMEM((2, chips, t, COLS), jnp.float32),
+            pltpu.VMEM((2, 2, t, LANES), jnp.float32),
+            pltpu.VMEM((2, 2, t, COLS), jnp.float32),
+            dma((el,)), dma((4,)), dma((2,)),
+            dma((2,)), dma((2,)), dma((3, 2)), dma((2, 2)), dma((3, 2)), dma((2, 2)),
+            reg, reg((2,)), reg((2,)),
+        ],
+        compiler_params=pltpu.CompilerParams(vmem_limit_bytes=VMEM_LIMIT, collective_id=0, has_side_effects=True),
+        cost_estimate=pl.CostEstimate(flops=2 * el * n * f * d + 6 * g * n * t * d, bytes_accessed=60_000_000, transcendentals=0),
+        name='down',
+    )(he, ue2, hit, gr)
 
 
 def solution(mesh):
@@ -83,17 +371,16 @@
         ne = el * g_
         t = b * s
         cap = CAP_FACTOR * t * top // ne
+        u = _rms(h0, ln_moe).reshape(t, d)
+        meta = jnp.zeros((16, d), jnp.bfloat16)
+        meta = meta.at[0:top, :t].set(idx.reshape(t, top).T.astype(jnp.bfloat16))
+        meta = meta.at[8:8 + top, :t].set(slot.reshape(t, top).T.astype(jnp.bfloat16))
+        ug = lax.all_gather(jnp.concatenate([u, meta], axis=0), 'ep')
         a, fo = _dense(h0, ln_attn, wq, wk, wv, wo, ln_ffn, ws1, ws3, ws2)
-        u = _rms(h0, ln_moe).reshape(t, d)
-        gi = idx.reshape(t, top)
-        sl = slot.reshape(t, top)
-        gate = _gate(u, wr, gi)
-        disp, comb = _route(gi * cap + sl, gate, ne * cap)
-        send = _mm('tr,td->rd', disp, u).astype(jnp.bfloat16).reshape(g_, el, cap, d)
-        recv = lax.all_to_all(send, 'ep', 0, 0, tiled=True)
-        y = _experts(recv, ue1, ue3, ue2)
-        back = lax.all_to_all(y, 'ep', 0, 0, tiled=True).reshape(ne * cap, d)
-        m = sum(_mm('tr,rd->td', p, back) for p in _parts(comb))
+        base = (lax.axis_index('ep') * (el * cap)).astype(jnp.int32).reshape(1)
+        x, hit, gr = _dispatch(base, ug, wr, el, cap, top)
+        he = _up(x.reshape(el, g_ * cap, d), ue1, ue3)
+        m = _down(he, ue2, hit, gr, g_)
         out = a.astype(jnp.float32) + fo + m.reshape(b, s, d)
         return out.astype(jnp.bfloat16)
 

time: 891 us -> 482 us (0.54)
  Pallas kernels: 0 us -> 316 us
  blocking collectives: 285 us -> 0 us
  matrix products: 341 us -> 82.2 us
  waiting for transfers between devices: 148 us -> 0.06 us
  other arithmetic: 51.8 us -> 31.5 us
  local copies, waits for them, and re-layouts: 50.9 us -> 31.3 us
  between operations: 0.52 us -> 14.1 us
    pallas_call x0 -> x3, Pallas kernels: none -> 316 us  [the longest x1 176 us: _down(): pl.pallas_call(lambda *refs: _down_kernel(nc, g, *refs), in_specs=[pl.Blo...]
    all_to_all x1 -> x0, blocking collectives: 285 us -> none  [local(): recv = lax.all_to_all(send, 'ep', 0, 0, tiled=True)]
    dot_general x16 -> x8, matrix products: 341 us -> 82.2 us  [_mm(): return jnp.einsum(form, a, b, preferred_element_type=jnp.float32)]
    all_to_all x1 -> x0, waiting for transfers between devices: 148 us -> none  [local(): back = lax.all_to_all(y, 'ep', 0, 0, tiled=True).reshape(ne * cap, d)]
    convert_element_type x1 -> x0, local copies, waits for them, and re-layouts: 21 us -> none  [_experts(): return _mm('egcf,efd->gecd', he, ue2).astype(jnp.bfloat16)]
    reduce_sum x3 -> x0, other arithmetic: 18.2 us -> none  [the longest x1 18.1 us: _route(): comb = jnp.sum(jnp.where(hit, gate[..., None], 0.0), axis=-2)]
    reduce_or x1 -> x0, other arithmetic: 11.1 us -> none  [_route(): disp = jnp.any(hit, axis=-2).astype(jnp.bfloat16)]
  transfers between devices with their start and end apart: 1 -> 1, of which waited for: 1 -> 0; matrix products, arithmetic and copies ran while one was open for 14% -> 23% of each run, Pallas kernels for 0% -> 0%
where the time goes in v1:
time: 482 us; the launch traced here: 475 us
  Pallas kernels  316 us (66%)
  matrix products  82.2 us (17%)
  other arithmetic  31.5 us (7%)
  local copies, waits for them, and re-layouts  31.3 us (6%)
  between operations  14.1 us (3%)
    pallas_call x1, Pallas kernels, _down(): pl.pallas_call(lambda *refs: _down_kernel(nc, g, *refs), in_specs=[pl.Blo...  176 us
    pallas_call x1, Pallas kernels, _up(): pl.pallas_call(_up_kernel, grid=(el,), in_specs=[pl.BlockSpec((1, n, d),...  95.3 us
    dot_general x8, matrix products, _mm(): return jnp.einsum(form, a, b, preferred_element_type=jnp.float32)  82.2 us
    pallas_call x1, Pallas kernels, _dispatch(): pl.pallas_call(lambda *refs: _dispatch_kernel(el, cap, top, *refs), grid=...  44.6 us
    dot_general x2, local copies, waits for them, and re-layouts, _mm(): return jnp.einsum(form, a, b, preferred_element_type=jnp.float32)  24.7 us
    sub x1, other arithmetic, _dense(): jax.nn.softmax(jnp.where(causal, sc, -1e+30), axis=-1).astype(jnp.bfloat16)  18.2 us
  transfers between devices with their start and end apart: 1, of which 0 were waited for; matrix products, arithmetic and copies ran while one was open for 23% of the time, Pallas kernels for 0%

profile of v1, /device:TPU:81, one launch (start us, length us, event | category | flops | bytes accessed | tf_op | source)
XLA Modules:
  0.0 475.5 jit_solution(12078432791271978120)
XLA Ops:
  6.5 0.0 all-gather.3.cloned.1.call-start
  6.6 2.1 fusion.10
  8.6 0.7 fusion.39
  9.4 0.7 fusion.40
  10.1 0.7 convert_element_type.93
  10.8 3.5 fusion.18
  14.2 0.0 copy-start.4
  14.2 0.0 copy-start
  14.2 0.4 scatter.9
  14.6 3.4 pad_maximum_fusion
  18.0 0.1 all-gather.3.cloned.1.call-update
  18.1 0.0 copy-done.4
  18.1 0.0 copy-done
  18.1 9.2 %convolution_convert_fusion = bf16[512,2048]{1,0:T(8,128)(2,1)} fusion(bf16[2048,2048]{1,0:T(8,128)(2,1)} %param.27, bf16[1,512,2048]{2,1,0:T(8,128)(2,1)S(1)} %copy-done, f32[2048]{0:T(1024)S(1)} %convert_element_type.81, f32[512]{0:T(512)S(1)} %add_rsqrt_fusion.1), kind=kOutput, calls=%fused_computation.27 | convolution fusion | flops 4300210176 | bytes 12593152 | tf_op jit(solution)/shard_map/bsd,de->bse/dot_general | solution.py:14
  27.3 3.9 copy.30
  31.3 12.3 %copy.32 = bf16[2048,2048]{1,0:T(8,128)(2,1)} copy(bf16[2048,2048]{0,1:T(8,128)(2,1)} %bitcast.71) | data formatting | bytes 16777216 | tf_op jit(solution)/shard_map/bsd,de->bse/dot_general | solution.py:14
  43.5 0.0 copy-start.1
  43.5 0.0 copy-start.5
  43.5 12.4 %copy.31 = bf16[2048,2048]{1,0:T(8,128)(2,1)} copy(bf16[2048,2048]{0,1:T(8,128)(2,1)} %bitcast.72) | data formatting | bytes 16777216 | tf_op jit(solution)/shard_map/bsd,de->bse/dot_general | solution.py:14
  55.9 0.0 copy-done.1
  55.9 1.0 copy.26.refs_2_
  56.9 0.0 copy-done.5
  56.9 0.0 copy-start.2
  57.0 0.0 slice-start
  57.0 0.1 iota_compare_fusion
  57.1 0.5 fusion.38
  57.6 0.0 slice-start.1
  57.6 7.6 %convolution_bitcast_fusion = f32[1,512,16,128]{1,3,2,0:T(8,128)S(1)} fusion(bf16[16,128,2048]{2,1,0:T(8,128)(2,1)} %bitcast.76, bf16[1,512,2048]{2,1,0:T(8,128)(2,1)S(1)} %copy-done, f32[2048]{0:T(1024)S(1)} %convert_element_type.81, f32[512]{0:T(512)S(1)} %add_rsqrt_fusion.1), kind=kOutput, calls=%fused_computation.29 | convolution fusion | flops 4299161600 | bytes 14690304 | tf_op jit(solution)/shard_map/bsd,de->bse/dot_general | solution.py:14
  65.2 0.0 slice-done
  65.2 0.0 slice-done.1
  65.3 4.7 convolution_bitcast_fusion.1
  70.0 1.5 fusion.32
  71.5 8.2 %fusion.19 = f32[16,512,512]{1,2,0:T(8,128)} fusion(bf16[512,16,64]{0,2,1:T(8,128)(2,1)S(1)} %get-tuple-element.39, bf16[512,16,64]{0,2,1:T(8,128)(2,1)S(1)} %get-tuple-element.40, bf16[512,16,64]{0,2,1:T(8,128)(2,1)S(1)} %get-tuple-element.36, bf16[512,16,64]{0,2,1:T(8,128)(2,1)S(1)} %get-tuple-element.35), kind=kOutput, calls=%fused_computation.33 | convolution fusion | flops 1082130432 | bytes 20971520 | tf_op jit(solution)/shard_map/bqhe,bkhe->bhqk/dot_general | solution.py:14
  79.7 18.2 %fusion.47 = (f32[16,512]{1,0:T(8,128)S(1)}, f32[16,512,512]{1,2,0:T(8,128)}) fusion(f32[16,512,512]{1,2,0:T(8,128)} %fusion.19, pred[512,512]{0,1:T(8,128)(4,1)S(1)} %iota_compare_fusion), kind=kOutput, calls=%fused_computation.67 | output fusion | flops 25166336 | bytes 33849344 | tf_op jit(solution)/shard_map/sub | solution.py:42
  97.9 7.7 %fusion.29 = bf16[16,128,512]{2,1,0:T(8,128)(2,1)S(1)} fusion(bf16[512,16,128]{0,2,1:T(8,128)(2,1)} %bitcast.77, f32[16,512,512]{1,2,0:T(8,128)} %get-tuple-element.44, f32[16,512]{1,0:T(8,128)S(1)} %get-tuple-element.43), kind=kOutput, calls=%fused_computation.47 | convolution fusion | flops 1083179008 | bytes 21004288 | tf_op jit(solution)/shard_map/bhqk,bkhe->bqhe/dot_general | solution.py:14
  105.6 8.4 %fusion.12 = (f32[512]{0:T(512)S(1)}, bf16[1,512,2048]{2,1,0:T(8,128)(2,1)S(1)}) fusion(bf16[512,2048]{0,1:T(8,128)(2,1)S(1)} %bitcast.80, bf16[2048,2048]{1,0:T(8,128)(2,1)} %param.28, bf16[1,512,2048]{2,1,0:T(8,128)(2,1)S(1)} %copy-done), kind=kOutput, calls=%fused_computation.22 | convolution fusion | flops 4301258240 | bytes 14682112 | tf_op jit(solution)/shard_map/bse,ed->bsd/dot_general | solution.py:14
  114.1 0.0 copy-start.8
  114.1 0.0 copy-start.6
  114.1 0.0 copy-done.2
  114.1 1.3 copy-done.8
  115.4 0.0 copy-done.6
  115.4 11.2 %fusion.35 = f32[512,2816]{1,0:T(8,128)} fusion(bf16[2048,2816]{1,0:T(8,128)(2,1)} %param.30, bf16[1,512,2048]{2,1,0:T(8,128)(2,1)S(1)} %get-tuple-element.46, f32[2048]{0:T(1024)S(1)} %convert_element_type.90, f32[512]{0:T(512)S(1)} %add_rsqrt_fusion), kind=kOutput, calls=%fused_computation.53 | convolution fusion | flops 5909774336 | bytes 19408896 | tf_op jit(solution)/shard_map/bsd,df->bsf/dot_general | solution.py:14
  126.6 0.0 all-gather.3.cloned.1.call-done
  126.6 44.6 %dispatch.1 = (bf16[8,8,96,2048]{3,2,1,0:T(8,128)(2,1)}, bf16[8,768,512]{2,1,0:T(8,128)(2,1)}, f32[8,768,128]{2,1,0:T(8,128)}) custom-call(s32[1]{0:T(128)} %bitcast.19.refs_0_, bf16[8,528,2048]{2,1,0:T(8,128)(2,1)} %bitcast.78, bf16[2048,64]{1,0:T(8,128)(2,1)} %copy.26.refs_2_), custom_call_target="tpu_custom_call" | custom-call | flops 12884901888 | bytes 60000000 | tf_op jit(solution)/shard_map/dispatch/pallas_call | solution.py:98
  171.2 95.3 %up.1.refs_0_ = bf16[8,768,1408]{2,1,0:T(8,128)(2,1)} custom-call(bf16[8,768,2048]{2,1,0:T(8,128)(2,1)} %bitcast.79, bf16[8,2048,1408]{2,1,0:T(8,128)(2,1)} %w1_ref.1, bf16[8,2048,1408]{2,1,0:T(8,128)(2,1)} %w3_ref.1), custom_call_target="tpu_custom_call" | custom-call | flops 70866960384 | bytes 100000000 | tf_op jit(solution)/shard_map/up/pallas_call | solution.py:136
  266.5 0.0 copy-start.3
  266.5 0.0 copy-start.7
  266.5 176.5 %down.1 = f32[512,2048]{1,0:T(8,128)} custom-call(bf16[8,768,1408]{2,1,0:T(8,128)(2,1)} %up.1.refs_0_, bf16[8,1408,2048]{2,1,0:T(8,128)(2,1)} %refs_1_.1, bf16[8,768,512]{2,1,0:T(8,128)(2,1)} %get-tuple-element.33.refs_2_, f32[8,768,128]{2,1,0:T(8,128)} %get-tuple-element.34.refs_3_), custom_call_target="tpu_custom_call" | custom-call | flops 74088185856 | bytes 60000000 | tf_op jit(solution)/shard_map/down/pallas_call | solution.py:337
  443.0 0.0 copy-done.3
  443.0 0.0 copy-done.7
  443.0 25.2 %fusion.16 = bf16[1,512,2048]{2,1,0:T(8,128)(2,1)} fusion(bf16[1,512,2048]{2,1,0:T(8,128)(2,1)} %copy-done.8, f32[512,2048]{1,0:T(8,128)} %down.1, bf16[2816,2048]{1,0:T(8,128)(2,1)} %param.32, f32[512,2816]{1,0:T(8,128)} %fusion.35, bf16[2048,2816]{1,0:T(8,128)(2,1)} %param.31, f32[2048]{0:T(1024)S(1)} %copy-done.3, f32[512]{0:T(512)S(1)} %copy-done.7), kind=kOutput, calls=%fused_computation.26 | convolution fusion | flops 11828199424 | bytes 37234688 | tf_op jit(solution)/shard_map/bsf,fd->bsd/dot_general | solution.py:14
  (7 shorter events, 0.0 us)
Async XLA Ops:
  6.5 120.1 %all-gather.3.cloned.1.call-start = ((), (), s32[]{:S(2)}) async-start(), calls=%async_computation | async-start | bytes 19464192 | tf_op jit(solution)/shard_map/all_gather | solution.py:378
  14.2 3.9 copy-start.4
  14.2 3.9 copy-start
  43.5 12.4 %copy-start.1 = (bf16[2048,64]{0,1:T(8,128)(2,1)S(1)}, bf16[2048,64]{0,1:T(8,128)(2,1)}, u32[]{:S(2)}) copy-start(bf16[2048,64]{0,1:T(8,128)(2,1)} %param.34) | copy-start | bytes 786436
  43.5 13.4 %copy-start.5 = (bf16[2048]{0:T(1024)(128)(2,1)S(1)}, bf16[2048]{0:T(1024)(128)(2,1)}, u32[]{:S(2)}) copy-start(bf16[2048]{0:T(1024)(128)(2,1)} %param.29) | copy-start | bytes 12292
  56.9 57.1 %copy-start.2 = (f32[2048]{0:T(1024)}, f32[2048]{0:T(1024)S(1)}, u32[]{:S(2)}) copy-start(f32[2048]{0:T(1024)S(1)} %convert_element_type.90) | copy-start | bytes 24580
  57.0 8.3 %slice-start = ((s8[8388608]{0:T(1024)(128)(4,1)}), s8[4194304]{0:T(1024)(128)(4,1)S(1)}, s32[]{:S(2)}) async-start(s8[8388608]{0:T(1024)(128)(4,1)} %bitcast.73), calls=%async_computation.1 | async-start | bytes 8388608
  57.6 7.6 %slice-start.1 = ((s8[8388608]{0:T(1024)(128)(4,1)}), s8[4194304]{0:T(1024)(128)(4,1)S(1)}, s32[]{:S(2)}) async-start(s8[8388608]{0:T(1024)(128)(4,1)} %bitcast.73), calls=%async_computation.2 | async-start | bytes 8388608
  114.1 1.4 copy-start.8
  114.1 1.3 copy-start.6
  266.5 176.5 %copy-start.3 = (f32[2048]{0:T(1024)S(1)}, f32[2048]{0:T(1024)}, u32[]{:S(2)}) copy-start(f32[2048]{0:T(1024)} %copy-done.2) | copy-start | bytes 24580
  266.5 176.5 %copy-start.7 = (f32[512]{0:T(512)S(1)}, f32[512]{0:T(512)}, u32[]{:S(2)}) copy-start(f32[512]{0:T(512)} %copy-done.6) | copy-start | bytes 6148
Sparse Core Ops, SparseCore 0:
  18.2 88.8 all-gather.2

commit v2 on v1

v2 whole, which is shorter than its diff:
```python
import jax
import jax.numpy as jnp
from jax import lax
from jax.experimental import pallas as pl
from jax.experimental.pallas import tpu as pltpu
from jax.sharding import PartitionSpec as P

HEAD = 128
EPS = 1e-6
CAP_FACTOR = 2


def _rms(x, w):
    xf = x.astype(jnp.float32)
    r = lax.rsqrt(jnp.mean(xf * xf, axis=-1, keepdims=True) + EPS)
    return (xf * r * w.astype(jnp.float32)).astype(jnp.bfloat16)


def _dot(a, b):
    return jnp.dot(a, b, preferred_element_type=jnp.float32)


def _angles(s):
    half = HEAD // 2
    freq = 10000.0 ** (-jnp.arange(half, dtype=jnp.float32) / half)
    ang = jnp.arange(s, dtype=jnp.float32)[:, None] * freq[None, :]
    c, sn = jnp.cos(ang), jnp.sin(ang)
    return jnp.concatenate([c, c], axis=1), jnp.concatenate([-sn, sn], axis=1)


def _attention_kernel(h_ref, ln_ref, cos_ref, sin_ref, wq_ref, wk_ref, wv_ref, o_ref, x_ref):
    s = h_ref.shape[0]
    block = s // 2

    @pl.when(pl.program_id(0) == 0)
    def _():
        x_ref[...] = _rms(h_ref[...], ln_ref[...])

    def rope(z):
        return (z * cos_ref[...] + pltpu.roll(z, HEAD // 2, 1) * sin_ref[...]).astype(jnp.bfloat16)

    q2, k2 = _dot(x_ref[...], wq_ref[...]), _dot(x_ref[...], wk_ref[...])
    v2 = _dot(x_ref[...], wv_ref[...]).astype(jnp.bfloat16)
    for h in range(q2.shape[1] // HEAD):
        cols = slice(h * HEAD, (h + 1) * HEAD)
        q, k, v = rope(q2[:, cols]), rope(k2[:, cols]), v2[:, cols]
        for b in range(2):
            n = (b + 1) * block
            sc = lax.dot_general(q[b * block:n], k[:n], (((1,), (1,)), ((), ())), preferred_element_type=jnp.float32)
            at = lax.broadcasted_iota(jnp.int32, (block, n), 0) + b * block
            sc = jnp.where(at >= lax.broadcasted_iota(jnp.int32, (block, n), 1), sc * HEAD ** -0.5, -1e30)
            e = jnp.exp(sc - jnp.max(sc, axis=1, keepdims=True))
            p = (e * (1.0 / jnp.sum(e, axis=1, keepdims=True))).astype(jnp.bfloat16)
            o_ref[b * block:n, cols] = _dot(p, v[:n]).astype(jnp.bfloat16)


def _attention(h, ln, wq, wk, wv):
    s, d = h.shape
    e = wq.shape[1]
    cos, sin = _angles(s)
    whole = lambda i: (0, 0)
    strip = pl.BlockSpec((d, 2 * HEAD), lambda i: (0, i))
    return pl.pallas_call(
        _attention_kernel,
        grid=(e // (2 * HEAD),),
        in_specs=[pl.BlockSpec((s, d), whole), pl.BlockSpec((1, d), whole), pl.BlockSpec((s, HEAD), whole),
                  pl.BlockSpec((s, HEAD), whole), strip, strip, strip],
        out_specs=pl.BlockSpec((s, 2 * HEAD), lambda i: (0, i)),
        out_shape=jax.ShapeDtypeStruct((s, e), jnp.bfloat16),
        scratch_shapes=[pltpu.VMEM((s, d), jnp.bfloat16)],
        compiler_params=pltpu.CompilerParams(vmem_limit_bytes=VMEM_LIMIT),
        cost_estimate=pl.CostEstimate(flops=6 * s * d * e + 4 * s * s * e, bytes_accessed=6 * d * e, transcendentals=0),
        name='attention',
    )(h, ln.reshape(1, d), cos, sin, wq, wk, wv)


def _ffn_kernel(n1, n2, h_ref, o_ref, ln_ref, wo_ref, w1_ref, w3_ref, w2_ref, out_ref, a_ref, x_ref, s_ref):
    i = pl.program_id(0)

    @pl.when(i < n1)
    def _():
        w = wo_ref.shape[1]
        cols = pl.ds(pl.multiple_of(i * w, w), w)
        a_ref[:, cols] = (h_ref[:, cols].astype(jnp.float32) + _dot(o_ref[...], wo_ref[...])).astype(jnp.bfloat16)

    @pl.when(i == n1)
    def _():
        x_ref[...] = _rms(a_ref[...], ln_ref[...])

    @pl.when(jnp.logical_and(i >= n1, i < n1 + n2))
    def _():
        w = w1_ref.shape[1]
        cols = pl.ds(pl.multiple_of((i - n1) * w, w), w)
        s_ref[:, cols] = (jax.nn.silu(_dot(x_ref[...], w1_ref[...])) * _dot(x_ref[...], w3_ref[...])).astype(jnp.bfloat16)

    @pl.when(i >= n1 + n2)
    def _():
        w = w2_ref.shape[1]
        cols = pl.ds(pl.multiple_of((i - n1 - n2) * w, w), w)
        out_ref[...] = a_ref[:, cols].astype(jnp.float32) + _dot(s_ref[...], w2_ref[...])


def _ffn(h, o, ln, wo, ws1, ws3, ws2):
    s, d = h.shape
    e, f = wo.shape[0], ws1.shape[1]
    c1, c2 = 512, 256
    n1, n2 = d // c1, f // c2
    whole = lambda i: (0, 0)
    clip = lambda x, hi: jnp.minimum(jnp.maximum(x, 0), hi)
    mid = pl.BlockSpec((d, c2), lambda i: (0, clip(i - n1, n2 - 1)))
    return pl.pallas_call(
        lambda *refs: _ffn_kernel(n1, n2, *refs),
        grid=(2 * n1 + n2,),
        in_specs=[pl.BlockSpec((s, d), whole), pl.BlockSpec((s, e), whole), pl.BlockSpec((1, d), whole),
                  pl.BlockSpec((e, c1), lambda i: (0, clip(i, n1 - 1))), mid, mid,
                  pl.BlockSpec((f, c1), lambda i: (0, clip(i - n1 - n2, n1 - 1)))],
        out_specs=pl.BlockSpec((s, c1), lambda i: (0, clip(i - n1 - n2, n1 - 1))),
        out_shape=jax.ShapeDtypeStruct((s, d), jnp.float32),
        scratch_shapes=[pltpu.VMEM((s, d), jnp.bfloat16), pltpu.VMEM((s, d), jnp.bfloat16), pltpu.VMEM((s, f), jnp.bfloat16)],
        compiler_params=pltpu.CompilerParams(vmem_limit_bytes=VMEM_LIMIT),
        cost_estimate=pl.CostEstimate(flops=2 * s * d * e + 6 * s * d * f, bytes_accessed=2 * d * e + 6 * d * f, transcendentals=0),
        name='ffn',
    )(h, o, ln.reshape(1, d), wo, ws1, ws3, ws2)


VMEM_LIMIT = 66_000_000
LANES = 128
COLS = 256
UE = 8
UD = 4
MESH = pl.DeviceIdType.MESH


def _dispatch_kernel(el, cap, top, base_ref, order_ref, ug_ref, wr_ref, x_ref, back_ref, gr_ref, hit_ref):
    t = hit_ref.shape[-1]
    ne = wr_ref.shape[-1]
    meta = ug_ref[0, t:t + 16, :t].astype(jnp.float32)
    idx = meta[0:top].astype(jnp.int32)
    row = idx * cap + meta[8:8 + top].astype(jnp.int32) - base_ref[0]
    lg = _dot(ug_ref[0, :t, :], wr_ref[...]).T
    expert = lax.broadcasted_iota(jnp.int32, (ne, t), 0)
    picked = [jnp.sum(jnp.where(expert == idx[j:j + 1], lg, 0.0), axis=0, keepdims=True) for j in range(top)]
    high = picked[0]
    for p in picked[1:]:
        high = jnp.maximum(high, p)
    ex = [jnp.exp(p - high) for p in picked]
    den = ex[0]
    for e in ex[1:]:
        den = den + e
    gate = [e / den for e in ex]
    col = jnp.concatenate([row, jnp.zeros((16 - top, t), jnp.int32)], axis=0).astype(jnp.float32).T.astype(jnp.int32)
    n = el * cap
    step, wide, blocks = 32, 2 * COLS, 2

    def build(r):
        at = lax.broadcasted_iota(jnp.int32, (step, t), 0) + r
        hit = jnp.zeros((step, t), jnp.float32)
        g = jnp.zeros((step, t), jnp.float32)
        for j in range(top):
            same = at == row[j:j + 1]
            hit = jnp.where(same, 1.0, hit)
            g = jnp.where(same, gate[j], g)
        hit_ref[r:r + step, :] = hit.astype(jnp.bfloat16)
        gr_ref[0, r:r + step, :] = jnp.broadcast_to(jnp.sum(g, axis=1, keepdims=True), (step, LANES))

    def build_back(r):
        at = lax.broadcasted_iota(jnp.int32, (step, n), 1)
        back = jnp.zeros((step, n), jnp.float32)
        for j in range(top):
            back = jnp.where(at == col[r:r + step, j:j + 1], 1.0, back)
        back_ref[0, r:r + step, :] = back.astype(jnp.bfloat16)

    part = n // blocks
    for h in range(blocks):
        for r in range(h * part, (h + 1) * part, step):
            build(r)
        for c in range(x_ref.shape[-1] // wide):
            cols = slice(c * wide, (c + 1) * wide)
            x = _dot(hit_ref[h * part:(h + 1) * part], ug_ref[0, :t, cols])
            x_ref[h * part // cap:(h + 1) * part // cap, 0, :, cols] = x.astype(jnp.bfloat16).reshape(part // cap, cap, wide)
    for r in range(0, t, step):
        build_back(r)


def _dispatch(base, order, ug, wr, el, cap, top):
    g = order.shape[0]
    _, rows, d = ug.shape
    t = rows - 16
    n = el * cap
    return pl.pallas_call(
        lambda *refs: _dispatch_kernel(el, cap, top, *refs),
        grid_spec=pltpu.PrefetchScalarGridSpec(
            num_scalar_prefetch=2,
            grid=(g,),
            in_specs=[
                pl.BlockSpec((1, rows, d), lambda i, base, order: (order[i], 0, 0)),
                pl.BlockSpec(wr.shape, lambda i, base, order: (0, 0)),
            ],
            out_specs=[
                pl.BlockSpec((el, 1, cap, d), lambda i, base, order: (0, i, 0, 0)),
                pl.BlockSpec((1, t, n), lambda i, base, order: (i, 0, 0)),
                pl.BlockSpec((1, n, LANES), lambda i, base, order: (i, 0, 0)),
            ],
            scratch_shapes=[pltpu.VMEM((n, t), jnp.bfloat16)],
        ),
        out_shape=[
            jax.ShapeDtypeStruct((el, g, cap, d), jnp.bfloat16),
            jax.ShapeDtypeStruct((g, t, n), jnp.bfloat16),
            jax.ShapeDtypeStruct((g, n, LANES), jnp.float32),
        ],
        compiler_params=pltpu.CompilerParams(vmem_limit_bytes=VMEM_LIMIT),
        cost_estimate=pl.CostEstimate(flops=2 * g * n * t * d, bytes_accessed=8_000_000 * g, transcendentals=0),
        name='dispatch',
    )(base, order, ug, wr)


def _up_kernel(x_ref, w1_ref, w3_ref, h_ref):
    for c in range(h_ref.shape[-1] // LANES):
        cols = slice(c * LANES, (c + 1) * LANES)
        r = _dot(x_ref[0], jnp.concatenate([w1_ref[0, :, cols], w3_ref[0, :, cols]], axis=1))
        h_ref[0, :, cols] = (jax.nn.silu(r[:, :LANES]) * r[:, LANES:]).astype(jnp.bfloat16)


def _up(x, ue1, ue3):
    el, n, d = x.shape
    f = ue1.shape[-1]
    return pl.pallas_call(
        _up_kernel,
        grid=(el,),
        in_specs=[
            pl.BlockSpec((1, n, d), lambda i: (i, 0, 0)),
            pl.BlockSpec((1, d, f), lambda i: (i, 0, 0)),
            pl.BlockSpec((1, d, f), lambda i: (i, 0, 0)),
        ],
        out_specs=pl.BlockSpec((1, n, f), lambda i: (i, 0, 0)),
        out_shape=jax.ShapeDtypeStruct((el, n, f), jnp.bfloat16),
        compiler_params=pltpu.CompilerParams(vmem_limit_bytes=VMEM_LIMIT),
        cost_estimate=pl.CostEstimate(flops=4 * el * n * f * d, bytes_accessed=100_000_000, transcendentals=0),
        name='up',
    )(x, ue1, ue3)


def _down_kernel(nc, g, he_hbm, w_hbm, hit_hbm, gr_hbm, out_ref,
                 he, w, hit, gr, y, p, ra, rb, rf,
                 he_sem, w_sem, in_sem, a_send, a_recv, b_send, b_recv, f_send, f_recv, a_free, b_free, f_free, out_sem):
    el, n, f = he.shape
    t = hit.shape[1]
    cap = n // g
    chips = g // 2
    me = lax.axis_index('ep')
    core, chip = lax.rem(me, 2), lax.div(me, 2)
    mate = me + 1 - 2 * core
    left, right = 2 * lax.rem(chip + chips - 1, chips) + core, 2 * lax.rem(chip + 1, chips) + core
    lchip, rchip, ochip, chip, core = chips - 1, 1, chips // 2, 0, 0

    def he_copy(e):
        return pltpu.make_async_copy(he_hbm.at[e], he.at[e], he_sem.at[e])

    def w_copy(q):
        e, c = lax.rem(q, el), lax.div(q, el)
        cols = pl.ds(pl.multiple_of(c * COLS, COLS), COLS)
        return pltpu.make_async_copy(w_hbm.at[e, :, cols], w.at[lax.rem(c, 2), e], w_sem.at[lax.rem(c, 2), e])

    in_copies = [pltpu.make_async_copy(hit_hbm, hit, in_sem.at[0]), pltpu.make_async_copy(gr_hbm, gr, in_sem.at[1])]

    def a_copy(c):
        return pltpu.make_async_remote_copy(
            src_ref=p.at[lax.rem(c, 3), 1], dst_ref=ra.at[lax.rem(c, 2)],
            send_sem=a_send.at[lax.rem(c, 2)], recv_sem=a_recv.at[lax.rem(c, 2)],
            device_id={'ep': mate}, device_id_type=MESH)

    def b_copy(c, way):
        return pltpu.make_async_remote_copy(
            src_ref=p.at[lax.rem(c, 3), 0, ochip, :, pl.ds(way * LANES, LANES)], dst_ref=rb.at[lax.rem(c, 2), way],
            send_sem=b_send.at[lax.rem(c, 2), way], recv_sem=b_recv.at[lax.rem(c, 2), way],
            device_id={'ep': (left, right)[way]}, device_id_type=MESH)

    def f_copy(c, way):
        return pltpu.make_async_remote_copy(
            src_ref=p.at[lax.rem(c, 3), 0, (lchip, rchip)[way]], dst_ref=rf.at[lax.rem(c, 2), way],
            send_sem=f_send.at[lax.rem(c, 2), way], recv_sem=f_recv.at[lax.rem(c, 2), way],
            device_id={'ep': (left, right)[way]}, device_id_type=MESH)

    def signal(sem, dev):
        pl.semaphore_signal(sem, inc=1, device_id={'ep': dev}, device_id_type=MESH)

    for e in range(el):
        w_copy(e).start()
        he_copy(e).start()
    for copy in in_copies:
        copy.start()

    barrier = pltpu.get_barrier_semaphore()
    for dev in (mate, left, right):
        signal(barrier, dev)
    pl.semaphore_wait(barrier, 3)

    def chunk(i, _):
        q0 = i * el

        @pl.when(i < nc)
        def _():
            @pl.when(i == 0)
            def _():
                for e in range(el):
                    he_copy(e).wait()
                for copy in in_copies:
                    copy.wait()

            @pl.when(i + 1 < nc)
            def _():
                for e in range(el):
                    w_copy(q0 + el + e).start()

            for e in range(el):
                w_copy(q0 + e).wait()

            def expert(e, _):
                q = q0 + e

                yy = jnp.dot(he[e], w[lax.rem(i, 2), e], preferred_element_type=jnp.float32)
                y[:, e] = yy.astype(jnp.bfloat16).reshape(g, cap, COLS)
                return 0

            lax.fori_loop(0, el, expert, 0, unroll=UE)


        @pl.when(jnp.logical_and(i >= 2, i <= nc + 1))
        def _():
            c = i - 2
            s, k = lax.rem(c, 3), lax.rem(c, 2)
            for way in range(2):
                b_copy(c, way).wait_recv()
                b_copy(c, way).wait_send()
            p[s, 0, lchip, :, :LANES] += rb[k, 0]
            p[s, 0, rchip, :, LANES:] += rb[k, 1]

            @pl.when(c < nc - 2)
            def _():
                signal(b_free.at[0], right)
                signal(b_free.at[1], left)

            @pl.when(c >= 2)
            def _():
                pl.semaphore_wait(f_free.at[0], 1)
                pl.semaphore_wait(f_free.at[1], 1)

            f_copy(c, 0).start()
            f_copy(c, 1).start()

        @pl.when(i >= 3)
        def _():
            c = i - 3
            s, k = lax.rem(c, 3), lax.rem(c, 2)
            f_copy(c, 0).wait_recv()
            f_copy(c, 1).wait_recv()
            rf[k, 0] = p[s, 0, 0] + (rf[k, 0] + rf[k, 1])
            f_copy(c, 0).wait_send()
            f_copy(c, 1).wait_send()
            cols = pl.ds(pl.multiple_of(c * COLS, COLS), COLS)
            done = pltpu.make_async_copy(rf.at[k, 0], out_ref.at[:, cols], out_sem)
            done.start()
            done.wait()

            @pl.when(c < nc - 2)
            def _():
                signal(f_free.at[0], right)
                signal(f_free.at[1], left)

        @pl.when(i < nc)
        def _():
            s = lax.rem(i, 3)

            def combine(side):
                def dest(dc, _):
                    dd = 2 * dc + side
                    scale = gr[dd]
                    z = y[dd].reshape(n, COLS).astype(jnp.float32) * jnp.concatenate([scale, scale], axis=1)
                    hi = z.astype(jnp.bfloat16)
                    z = z - hi.astype(jnp.float32)
                    mid = z.astype(jnp.bfloat16)
                    lo = (z - mid.astype(jnp.float32)).astype(jnp.bfloat16)
                    r = _dot(hit[dd], jnp.concatenate([hi, mid, lo], axis=1))
                    p[s, side, dc] = r[:, :COLS] + (r[:, COLS:2 * COLS] + r[:, 2 * COLS:])
                    return 0

                lax.fori_loop(0, chips, dest, 0, unroll=UD)

            combine(1)

            @pl.when(i >= 2)
            def _():
                pl.semaphore_wait(a_free, 1)

            a_copy(i).start()
            combine(0)
            cc = a_copy(i)
            cc.wait_recv()
            cc.wait_send()
            k = lax.rem(i, 2)
            p[s, 0, ochip] += ra[k, ochip]
            for r in (0, 1, chips - 1):
                p[s, 0, r] += ra[k, r]

            @pl.when(i < nc - 2)
            def _():
                signal(a_free, mate)

            @pl.when(i >= 2)
            def _():
                pl.semaphore_wait(b_free.at[0], 1)
                pl.semaphore_wait(b_free.at[1], 1)

            b_copy(i, 0).start()
            b_copy(i, 1).start()

        return 0

    lax.fori_loop(0, nc + 3, chunk, 0)


def _down(he, ue2, hit, gr):
    el, n, f = he.shape
    g, t, _ = hit.shape
    d = ue2.shape[-1]
    nc = d // COLS
    chips = g // 2
    dma = pltpu.SemaphoreType.DMA
    reg = pltpu.SemaphoreType.REGULAR
    return pl.pallas_call(
        lambda *refs: _down_kernel(nc, g, *refs),
        in_specs=[pl.BlockSpec(memory_space=pl.ANY)] * 4,
        out_specs=pl.BlockSpec(memory_space=pl.ANY),
        out_shape=jax.ShapeDtypeStruct((t, d), jnp.float32),
        scratch_shapes=[
            pltpu.VMEM((el, n, f), jnp.bfloat16),
            pltpu.VMEM((2, el, f, COLS), jnp.bfloat16),
            pltpu.VMEM((g, t, n), jnp.bfloat16),
            pltpu.VMEM((g, n, LANES), jnp.float32),
            pltpu.VMEM((g, el, n // g, COLS), jnp.bfloat16),
            pltpu.VMEM((3, 2, chips, t, COLS), jnp.float32),
            pltpu.VMEM((2, chips, t, COLS), jnp.float32),
            pltpu.VMEM((2, 2, t, LANES), jnp.float32),
            pltpu.VMEM((2, 2, t, COLS), jnp.float32),
            dma((el,)), dma((2, el)), dma((2,)),
            dma((2,)), dma((2,)), dma((2, 2)), dma((2, 2)), dma((2, 2)), dma((2, 2)),
            reg, reg((2,)), reg((2,)), dma(()),
        ],
        compiler_params=pltpu.CompilerParams(vmem_limit_bytes=VMEM_LIMIT, collective_id=0, has_side_effects=True),
        cost_estimate=pl.CostEstimate(flops=2 * el * n * f * d + 6 * g * n * t * d, bytes_accessed=60_000_000, transcendentals=0),
        name='down',
    )(he, ue2, hit, gr)


def solution(mesh):
    g_ = mesh.shape['ep']
    rows = P(('dp', 'ep'))
    rep = P()

    def local(h0, idx, slot, ln_attn, wq, wk, wv, wo, ln_ffn, ws1, ws3, ws2, ln_moe, wr, ue1, ue3, ue2):
        b, s, d = h0.shape
        top = idx.shape[-1]
        el = ue1.shape[0]
        ne = el * g_
        t = b * s
        cap = CAP_FACTOR * t * top // ne
        u = _rms(h0, ln_moe).reshape(t, d)
        meta = jnp.zeros((16, d), jnp.bfloat16)
        meta = meta.at[0:top, :t].set(idx.reshape(t, top).T.astype(jnp.bfloat16))
        meta = meta.at[8:8 + top, :t].set(slot.reshape(t, top).T.astype(jnp.bfloat16))
        um = jnp.concatenate([u, meta], axis=0)
        ug = lax.all_gather(um, 'ep')
        h = h0.reshape(t, d)
        o = _attention(h, ln_attn, wq, wk, wv)
        dense = _ffn(h, o, ln_ffn, wo, ws1, ws3, ws2)
        me = lax.axis_index('ep')
        base = (me * (el * cap)).astype(jnp.int32).reshape(1)
        p = jnp.arange(g_)
        order = 2 * ((me // 2 + p // 2) % (g_ // 2)) + (me % 2 + p) % 2
        order = order.astype(jnp.int32)
        x, hit, gr = _dispatch(base, order, ug, wr, el, cap, top)
        he = _up(x.reshape(el, g_ * cap, d), ue1, ue3)
        m = _down(he, ue2, hit, gr)
        out = (dense + m).reshape(b, s, d)
        return out.astype(jnp.bfloat16)

    specs = (rows, rows, rows) + (rep,) * 11 + (P('ep'), P('ep'), P('ep'))
    return jax.shard_map(local, mesh=mesh, in_specs=specs, out_specs=rows, check_vma=False)
```

time: 482 us -> 402 us (0.83); the launches traced: 475 us -> 401 us
  matrix products: 82.2 us -> 0 us
  Pallas kernels: 316 us -> 355 us
  local copies, waits for them, and re-layouts: 31.3 us -> 2.7 us
  other arithmetic: 31.5 us -> 15.8 us
  waiting for transfers between devices: 0.06 us -> 13.9 us
    dot_general x8 -> x0, matrix products: 82.2 us -> none  [_mm(): return jnp.einsum(form, a, b, preferred_element_type=jnp.float32)]
    pallas_call x1 -> x3, Pallas kernels: 44.6 us -> 109 us  [the longest x1 38.6 us: _dispatch(): pl.pallas_call(lambda *refs: _dispatch_kernel(el, cap, top, *refs), grid_...]
    dot_general x2 -> x0, local copies, waits for them, and re-layouts: 24.7 us -> none  [_mm(): return jnp.einsum(form, a, b, preferred_element_type=jnp.float32)]
    sub x1 -> x0, other arithmetic: 18.2 us -> none  [_dense(): jax.nn.softmax(jnp.where(causal, sc, -1e+30), axis=-1).astype(jnp.bfloat16)]
    pallas_call x1, Pallas kernels: 95.3 us -> 79.6 us  [_up(): pl.pallas_call(_up_kernel, grid=(el,), in_specs=[pl.BlockSpec((1, n, d),...]
    all_gather x1, waiting for transfers between devices: 0.01 us -> 13.9 us  [local(): ug = lax.all_gather(um, 'ep')]
    pallas_call x1, Pallas kernels: 176 us -> 167 us  [_down(): pl.pallas_call(lambda *refs: _down_kernel(nc, g, *refs), in_specs=[pl.Blo...]
    convert_element_type x0 -> x1, other arithmetic: none -> 5.41 us  [local(): return out.astype(jnp.bfloat16)]
  transfers between devices with their start and end apart: 1 -> 1, of which waited for: 0 -> 1; matrix products, arithmetic and copies ran while one was open for 23% -> 1% of each run, Pallas kernels for 0% -> 18%
where the time goes in v2:
time: 402 us; the launch traced here: 401 us
  Pallas kernels  355 us (88%)
  other arithmetic  15.8 us (4%)
  waiting for transfers between devices  13.9 us (3%)
  between operations  13.5 us (3%)
    pallas_call x1, Pallas kernels, _down(): pl.pallas_call(lambda *refs: _down_kernel(nc, g, *refs), in_specs=[pl.Blo...  167 us
    pallas_call x1, Pallas kernels, _up(): pl.pallas_call(_up_kernel, grid=(el,), in_specs=[pl.BlockSpec((1, n, d),...  79.6 us
    pallas_call x1, Pallas kernels, _dispatch(): pl.pallas_call(lambda *refs: _dispatch_kernel(el, cap, top, *refs), grid_...  38.6 us
    pallas_call x1, Pallas kernels, _attention(): pl.pallas_call(_attention_kernel, grid=(e // (2 * HEAD),), in_specs=[pl.B...  35.4 us
    pallas_call x1, Pallas kernels, _ffn(): pl.pallas_call(lambda *refs: _ffn_kernel(n1, n2, *refs), grid=(2 * n1 + n...  34.9 us
    all_gather x1, waiting for transfers between devices, local(): ug = lax.all_gather(um, 'ep')  13.9 us
  transfers between devices with their start and end apart: 1, of which 1 were waited for; matrix products, arithmetic and copies ran while one was open for 1% of the time, Pallas kernels for 18%

profile of v2, /device:TPU:81, one launch (start us, length us, event | category | flops | bytes accessed | tf_op | source)
XLA Modules:
  0.0 401.3 jit_solution(11769961888725724912)
XLA Ops:
  6.5 0.0 all-gather.3.cloned.1.call-start
  6.6 0.7 convert_element_type.34
  7.2 2.1 fusion
  9.3 0.7 convert_element_type.36
  10.1 0.7 convert_element_type.39
  10.8 2.1 fusion.4
  12.9 0.0 copy-start
  13.0 0.0 copy-start.1
  13.0 0.0 copy-start.2
  13.0 0.5 scatter.9
  13.5 1.5 pad_maximum_fusion
  15.0 0.1 all-gather.3.cloned.1.call-update
  15.1 0.0 copy-done
  15.1 1.0 copy.18.refs_3_
  16.1 0.0 copy-done.1
  16.1 0.6 reshape.108.ln_ref
  16.7 0.0 copy-done.2
  16.7 0.6 reshape.109.refs_2_
  17.3 0.5 fusion.8.refs_1_
  17.8 1.0 fusion.7
  18.8 1.0 pad_maximum_fusion.1
  19.8 35.4 %attention.1.refs_1_ = bf16[512,2048]{1,0:T(8,128)(2,1)} custom-call(bf16[512,2048]{1,0:T(8,128)(2,1)} %bitcast.18, bf16[1,2048]{1,0:T(2,128)(2,1)} %reshape.108.ln_ref, f32[512,128]{1,0:T(8,128)} %get-tuple-element.38.cos_ref, f32[512,128]{1,0:T(8,128)} %get-tuple-element.39.sin_ref, bf16[2048,2048]{1,0:T(8,128)(2,1)} %wq_ref.1, bf16[2048,2048]{1,0:T(8,128)(2,1)} %wk_ref.1, ...), custom_call_target="tpu_custom_call" | custom-call | flops 15032385536 | bytes 25165824 | tf_op jit(solution)/shard_map/attention/pallas_call | solution.py:63
  55.3 34.9 %ffn.1 = f32[512,2048]{1,0:T(8,128)} custom-call(bf16[512,2048]{1,0:T(8,128)(2,1)} %bitcast.19, bf16[512,2048]{1,0:T(8,128)(2,1)} %attention.1.refs_1_, bf16[1,2048]{1,0:T(2,128)(2,1)} %reshape.109.refs_2_, bf16[2048,2048]{1,0:T(8,128)(2,1)} %refs_3_.2, bf16[2048,2816]{1,0:T(8,128)(2,1)} %refs_4_.1, bf16[2048,2816]{1,0:T(8,128)(2,1)} %refs_5_.1, ...), custom_call_target="tpu_custom_call" | custom-call | flops 22011707392 | bytes 42991616 | tf_op jit(solution)/shard_map/ffn/pallas_call | solution.py:111
  90.2 13.9 %all-gather.3.cloned.1.call-done = bf16[4224,2048]{1,0:T(8,128)(2,1)} async-done(((bf16[528,2048]{1,0:T(8,128)(2,1)}), bf16[4224,2048]{1,0:T(8,128)(2,1)}) %all-gather.3.cloned.1.call-update) | async-done | bytes 17301520 | tf_op jit(solution)/shard_map/all_gather | solution.py:472
  104.1 38.6 %dispatch.1 = (bf16[8,8,96,2048]{3,2,1,0:T(8,128)(2,1)}, bf16[8,512,768]{2,1,0:T(8,128)(2,1)}, f32[8,768,128]{2,1,0:T(8,128)}) custom-call(s32[1]{0:T(128)} %bitcast.1.refs_0_, s32[8]{0:T(128)} %fusion.8.refs_1_, bf16[8,528,2048]{2,1,0:T(8,128)(2,1)} %bitcast.22, bf16[2048,64]{1,0:T(8,128)(2,1)} %copy.18.refs_3_), custom_call_target="tpu_custom_call" | custom-call | flops 12884901888 | bytes 64000000 | tf_op jit(solution)/shard_map/dispatch/pallas_call | solution.py:190
  142.6 79.6 %up.1.refs_0_ = bf16[8,768,1408]{2,1,0:T(8,128)(2,1)} custom-call(bf16[8,768,2048]{2,1,0:T(8,128)(2,1)} %bitcast.23, bf16[8,2048,1408]{2,1,0:T(8,128)(2,1)} %w1_ref.1, bf16[8,2048,1408]{2,1,0:T(8,128)(2,1)} %w3_ref.1), custom_call_target="tpu_custom_call" | custom-call | flops 70866960384 | bytes 100000000 | tf_op jit(solution)/shard_map/up/pallas_call | solution.py:227
  222.2 166.8 %down.1 = f32[512,2048]{1,0:T(8,128)} custom-call(bf16[8,768,1408]{2,1,0:T(8,128)(2,1)} %up.1.refs_0_, bf16[8,1408,2048]{2,1,0:T(8,128)(2,1)} %refs_1_.1, bf16[8,512,768]{2,1,0:T(8,128)(2,1)} %get-tuple-element.33.refs_2_, f32[8,768,128]{2,1,0:T(8,128)} %get-tuple-element.34.refs_3_), custom_call_target="tpu_custom_call" | custom-call | flops 74088185856 | bytes 60000000 | tf_op jit(solution)/shard_map/down/pallas_call | solution.py:430
  389.0 5.4 %fusion.3 = bf16[1,512,2048]{2,1,0:T(8,128)(2,1)} fusion(f32[512,2048]{1,0:T(8,128)} %ffn.1, f32[512,2048]{1,0:T(8,128)} %down.1), kind=kLoop, calls=%fused_computation.7 | loop fusion | flops 2097152 | bytes 10485760 | tf_op jit(solution)/shard_map/convert_element_type | solution.py:485
  (5 shorter events, 0.0 us)
Async XLA Ops:
  6.5 97.5 %all-gather.3.cloned.1.call-start = ((), (), s32[]{:S(2)}) async-start(), calls=%async_computation | async-start | bytes 19464192 | tf_op jit(solution)/shard_map/all_gather | solution.py:472
  12.9 2.1 copy-start
  13.0 3.1 copy-start.1
  13.0 3.7 copy-start.2
Sparse Core Ops, SparseCore 0:
  15.2 88.8 all-gather.2

commit v3 on v2

--- a/solution.py
+++ b/solution.py
@@ -131,6 +131,25 @@
 MESH = pl.DeviceIdType.MESH
 
 
+def _prepare_kernel(h_ref, ln_ref, meta_ref, um_ref):
+    t, d = h_ref.shape
+    m = meta_ref.shape[0]
+    um_ref[:t, :] = _rms(h_ref[...], ln_ref[...])
+    um_ref[t:, :] = jnp.zeros((m, d), jnp.bfloat16)
+    um_ref[t:, :t] = meta_ref[...]
+
+
+def _prepare(h, ln, meta):
+    t, d = h.shape
+    return pl.pallas_call(
+        _prepare_kernel,
+        out_shape=jax.ShapeDtypeStruct((t + meta.shape[0], d), jnp.bfloat16),
+        compiler_params=pltpu.CompilerParams(vmem_limit_bytes=16_000_000),
+        cost_estimate=pl.CostEstimate(flops=4 * t * d, bytes_accessed=4 * t * d, transcendentals=0),
+        name='prepare',
+    )(h, ln.reshape(1, d), meta)
+
+
 def _dispatch_kernel(el, cap, top, base_ref, order_ref, ug_ref, wr_ref, x_ref, back_ref, gr_ref, hit_ref):
     t = hit_ref.shape[-1]
     ne = wr_ref.shape[-1]
@@ -148,27 +167,31 @@
     for e in ex[1:]:
         den = den + e
     gate = [e / den for e in ex]
-    col = jnp.concatenate([row, jnp.zeros((16 - top, t), jnp.int32)], axis=0).astype(jnp.float32).T.astype(jnp.int32)
     n = el * cap
     step, wide, blocks = 32, 2 * COLS, 2
+    low = lax.broadcasted_iota(jnp.int32, (el, t), 0) * cap
+    mine = jnp.full((el, t), -1, jnp.int32)
+    scale = jnp.zeros((el, t), jnp.float32)
+    for j in range(top):
+        inside = jnp.logical_and(row[j:j + 1] >= low, row[j:j + 1] < low + cap)
+        mine = jnp.where(inside, row[j:j + 1], mine)
+        scale = jnp.where(inside, gate[j], scale)
+    col = jnp.concatenate([mine, mine], axis=0).astype(jnp.float32).T.astype(jnp.int32)
 
     def build(r):
-        at = lax.broadcasted_iota(jnp.int32, (step, t), 0) + r
-        hit = jnp.zeros((step, t), jnp.float32)
-        g = jnp.zeros((step, t), jnp.float32)
-        for j in range(top):
-            same = at == row[j:j + 1]
-            hit = jnp.where(same, 1.0, hit)
-            g = jnp.where(same, gate[j], g)
-        hit_ref[r:r + step, :] = hit.astype(jnp.bfloat16)
-        gr_ref[0, r:r + step, :] = jnp.broadcast_to(jnp.sum(g, axis=1, keepdims=True), (step, LANES))
+        e = r // cap
+        same = lax.broadcasted_iota(jnp.int32, (step, t), 0) + r == mine[e:e + 1]
+        hit_ref[r:r + step, :] = jnp.where(same, 1.0, 0.0).astype(jnp.bfloat16)
+        g = jnp.sum(jnp.where(same, scale[e:e + 1], 0.0), axis=1, keepdims=True)
+        gr_ref[0, r:r + step, :] = jnp.broadcast_to(g, (step, LANES))
 
     def build_back(r):
-        at = lax.broadcasted_iota(jnp.int32, (step, n), 1)
-        back = jnp.zeros((step, n), jnp.float32)
-        for j in range(top):
-            back = jnp.where(at == col[r:r + step, j:j + 1], 1.0, back)
-        back_ref[0, r:r + step, :] = back.astype(jnp.bfloat16)
+        for k in range(0, n, LANES):
+            at = lax.broadcasted_iota(jnp.int32, (LANES, LANES), 1) + k
+            back = jnp.zeros((LANES, LANES), jnp.float32)
+            for e in range(k // cap, (k + LANES - 1) // cap + 1):
+                back = jnp.where(at == col[r:r + LANES, e:e + 1], 1.0, back)
+            back_ref[0, r:r + LANES, k:k + LANES] = back.astype(jnp.bfloat16)
 
     part = n // blocks
     for h in range(blocks):
@@ -178,7 +201,7 @@
             cols = slice(c * wide, (c + 1) * wide)
             x = _dot(hit_ref[h * part:(h + 1) * part], ug_ref[0, :t, cols])
             x_ref[h * part // cap:(h + 1) * part // cap, 0, :, cols] = x.astype(jnp.bfloat16).reshape(part // cap, cap, wide)
-    for r in range(0, t, step):
+    for r in range(0, t, LANES):
         build_back(r)
 
 
@@ -240,9 +263,9 @@
     )(x, ue1, ue3)
 
 
-def _down_kernel(nc, g, he_hbm, w_hbm, hit_hbm, gr_hbm, out_ref,
+def _down_kernel(nc, g, he_hbm, w_hbm, hit_hbm, gr_hbm, dense_hbm, out_ref,
                  he, w, hit, gr, y, p, ra, rb, rf,
-                 he_sem, w_sem, in_sem, a_send, a_recv, b_send, b_recv, f_send, f_recv, a_free, b_free, f_free, out_sem):
+                 he_sem, w_sem, in_sem, a_send, a_recv, b_send, b_recv, f_send, f_recv, a_free, b_free, f_free, out_sem, dn, ob, dn_sem):
     el, n, f = he.shape
     t = hit.shape[1]
     cap = n // g
@@ -352,13 +375,16 @@
         def _():
             c = i - 3
             s, k = lax.rem(c, 3), lax.rem(c, 2)
+            cols = pl.ds(pl.multiple_of(c * COLS, COLS), COLS)
+            base = pltpu.make_async_copy(dense_hbm.at[:, cols], dn, dn_sem)
+            base.start()
             f_copy(c, 0).wait_recv()
             f_copy(c, 1).wait_recv()
-            rf[k, 0] = p[s, 0, 0] + (rf[k, 0] + rf[k, 1])
+            base.wait()
+            ob[...] = (dn[...] + (p[s, 0, 0] + (rf[k, 0] + rf[k, 1]))).astype(jnp.bfloat16)
             f_copy(c, 0).wait_send()
             f_copy(c, 1).wait_send()
-            cols = pl.ds(pl.multiple_of(c * COLS, COLS), COLS)
-            done = pltpu.make_async_copy(rf.at[k, 0], out_ref.at[:, cols], out_sem)
+            done = pltpu.make_async_copy(ob, out_ref.at[:, cols], out_sem)
             done.start()
             done.wait()
 
@@ -419,7 +445,7 @@
     lax.fori_loop(0, nc + 3, chunk, 0)
 
 
-def _down(he, ue2, hit, gr):
+def _down(he, ue2, hit, gr, dense):
     el, n, f = he.shape
     g, t, _ = hit.shape
     d = ue2.shape[-1]
@@ -429,9 +455,9 @@
     reg = pltpu.SemaphoreType.REGULAR
     return pl.pallas_call(
         lambda *refs: _down_kernel(nc, g, *refs),
-        in_specs=[pl.BlockSpec(memory_space=pl.ANY)] * 4,
+        in_specs=[pl.BlockSpec(memory_space=pl.ANY)] * 5,
         out_specs=pl.BlockSpec(memory_space=pl.ANY),
-        out_shape=jax.ShapeDtypeStruct((t, d), jnp.float32),
+        out_shape=jax.ShapeDtypeStruct((t, d), jnp.bfloat16),
         scratch_shapes=[
             pltpu.VMEM((el, n, f), jnp.bfloat16),
             pltpu.VMEM((2, el, f, COLS), jnp.bfloat16),
@@ -445,11 +471,12 @@
             dma((el,)), dma((2, el)), dma((2,)),
             dma((2,)), dma((2,)), dma((2, 2)), dma((2, 2)), dma((2, 2)), dma((2, 2)),
             reg, reg((2,)), reg((2,)), dma(()),
+            pltpu.VMEM((t, COLS), jnp.float32), pltpu.VMEM((t, COLS), jnp.bfloat16), dma(()),
         ],
         compiler_params=pltpu.CompilerParams(vmem_limit_bytes=VMEM_LIMIT, collective_id=0, has_side_effects=True),
         cost_estimate=pl.CostEstimate(flops=2 * el * n * f * d + 6 * g * n * t * d, bytes_accessed=60_000_000, transcendentals=0),
         name='down',
-    )(he, ue2, hit, gr)
+    )(he, ue2, hit, gr, dense)
 
 
 def solution(mesh):
@@ -464,11 +491,10 @@
         ne = el * g_
         t = b * s
         cap = CAP_FACTOR * t * top // ne
-        u = _rms(h0, ln_moe).reshape(t, d)
-        meta = jnp.zeros((16, d), jnp.bfloat16)
-        meta = meta.at[0:top, :t].set(idx.reshape(t, top).T.astype(jnp.bfloat16))
-        meta = meta.at[8:8 + top, :t].set(slot.reshape(t, top).T.astype(jnp.bfloat16))
-        um = jnp.concatenate([u, meta], axis=0)
+        pad = jnp.zeros((8 - top, t), jnp.bfloat16)
+        meta = jnp.concatenate([idx.reshape(t, top).T.astype(jnp.bfloat16), pad,
+                                slot.reshape(t, top).T.astype(jnp.bfloat16), pad], axis=0)
+        um = _prepare(h0.reshape(t, d), ln_moe, meta)
         ug = lax.all_gather(um, 'ep')
         h = h0.reshape(t, d)
         o = _attention(h, ln_attn, wq, wk, wv)
@@ -480,9 +506,8 @@
         order = order.astype(jnp.int32)
         x, hit, gr = _dispatch(base, order, ug, wr, el, cap, top)
         he = _up(x.reshape(el, g_ * cap, d), ue1, ue3)
-        m = _down(he, ue2, hit, gr)
-        out = (dense + m).reshape(b, s, d)
-        return out.astype(jnp.bfloat16)
+        out = _down(he, ue2, hit, gr, dense).reshape(b, s, d)
+        return out
 
     specs = (rows, rows, rows) + (rep,) * 11 + (P('ep'), P('ep'), P('ep'))
     return jax.shard_map(local, mesh=mesh, in_specs=specs, out_specs=rows, check_vma=False)

time: 402 us -> 386 us (0.960)
  other arithmetic: 15.8 us -> 3.3 us
  Pallas kernels: 355 us -> 346 us
  local copies, waits for them, and re-layouts: 2.7 us -> 9.95 us
    pallas_call x1, Pallas kernels: 38.6 us -> 27.4 us  [_dispatch(): pl.pallas_call(lambda *refs: _dispatch_kernel(el, cap, top, *refs), grid_...]
    convert_element_type x4 -> x1, other arithmetic: 7.54 us -> 0.73 us  [local(): idx.reshape(t, top).T.astype(jnp.bfloat16)]
    unnamed x9 -> x4, local copies, waits for them, and re-layouts: 1.03 us -> 6.68 us
  transfers between devices with their start and end apart: 1 -> 1, of which waited for: 1 -> 1; matrix products, arithmetic and copies ran while one was open for 1% -> 2% of each run, Pallas kernels for 18% -> 18%
where the time goes in v3:
time: 386 us; the launch traced here: 385 us
  Pallas kernels  346 us (90%)
  between operations  13.5 us (3%)
  waiting for transfers between devices  11.6 us (3%)
  local copies, waits for them, and re-layouts  9.95 us (3%)
    pallas_call x1, Pallas kernels, _down(): pl.pallas_call(lambda *refs: _down_kernel(nc, g, *refs), in_specs=[pl.Blo...  167 us
    pallas_call x1, Pallas kernels, _up(): pl.pallas_call(_up_kernel, grid=(el,), in_specs=[pl.BlockSpec((1, n, d),...  79.6 us
    pallas_call x1, Pallas kernels, _attention(): pl.pallas_call(_attention_kernel, grid=(e // (2 * HEAD),), in_specs=[pl.B...  35.4 us
    pallas_call x1, Pallas kernels, _ffn(): pl.pallas_call(lambda *refs: _ffn_kernel(n1, n2, *refs), grid=(2 * n1 + n...  34.9 us
    pallas_call x1, Pallas kernels, _dispatch(): pl.pallas_call(lambda *refs: _dispatch_kernel(el, cap, top, *refs), grid_...  27.4 us
    all_gather x1, waiting for transfers between devices, local(): ug = lax.all_gather(um, 'ep')  11.6 us
  transfers between devices with their start and end apart: 1, of which 1 were waited for; matrix products, arithmetic and copies ran while one was open for 2% of the time, Pallas kernels for 18%

profile of v3, /device:TPU:81, one launch (start us, length us, event | category | flops | bytes accessed | tf_op | source)
XLA Modules:
  0.0 384.7 jit_solution(2867364054268722443)
XLA Ops:
  6.5 0.0 all-gather.3.cloned.1.call-start
  6.6 0.7 reshape.34.ln_ref
  7.2 0.7 fusion.3
  8.0 0.0 copy-start
  8.0 1.6 copy-done
  9.6 2.2 prepare.1
  11.8 0.1 all-gather.3.cloned.1.call-update
  11.9 1.9 copy.20.refs_3_
  13.8 1.3 reshape.36.ln_ref
  15.1 1.3 reshape.37.refs_2_
  16.4 0.6 fusion.5.refs_1_
  16.9 1.0 fusion.2
  17.9 1.0 pad_maximum_fusion
  18.9 35.4 %attention.1.refs_1_ = bf16[512,2048]{1,0:T(8,128)(2,1)} custom-call(bf16[512,2048]{1,0:T(8,128)(2,1)} %bitcast.13, bf16[1,2048]{1,0:T(2,128)(2,1)} %reshape.36.ln_ref, f32[512,128]{1,0:T(8,128)} %get-tuple-element.16.cos_ref, f32[512,128]{1,0:T(8,128)} %get-tuple-element.17.sin_ref, bf16[2048,2048]{1,0:T(8,128)(2,1)} %wq_ref.1, bf16[2048,2048]{1,0:T(8,128)(2,1)} %wk_ref.1, ...), custom_call_target="tpu_custom_call" | custom-call | flops 15032385536 | bytes 25165824 | tf_op jit(solution)/shard_map/attention/pallas_call | solution.py:63
  54.4 34.9 %ffn.1.refs_4_ = f32[512,2048]{1,0:T(8,128)} custom-call(bf16[512,2048]{1,0:T(8,128)(2,1)} %bitcast.14, bf16[512,2048]{1,0:T(8,128)(2,1)} %attention.1.refs_1_, bf16[1,2048]{1,0:T(2,128)(2,1)} %reshape.37.refs_2_, bf16[2048,2048]{1,0:T(8,128)(2,1)} %refs_3_.2, bf16[2048,2816]{1,0:T(8,128)(2,1)} %refs_4_.1, bf16[2048,2816]{1,0:T(8,128)(2,1)} %refs_5_.1, ...), custom_call_target="tpu_custom_call" | custom-call | flops 22011707392 | bytes 42991616 | tf_op jit(solution)/shard_map/ffn/pallas_call | solution.py:111
  89.3 11.6 %all-gather.3.cloned.1.call-done = bf16[4224,2048]{1,0:T(8,128)(2,1)} async-done(((bf16[528,2048]{1,0:T(8,128)(2,1)}), bf16[4224,2048]{1,0:T(8,128)(2,1)}) %all-gather.3.cloned.1.call-update) | async-done | bytes 17301520 | tf_op jit(solution)/shard_map/all_gather | solution.py:498
  100.8 27.4 %dispatch.1 = (bf16[8,8,96,2048]{3,2,1,0:T(8,128)(2,1)}, bf16[8,512,768]{2,1,0:T(8,128)(2,1)}, f32[8,768,128]{2,1,0:T(8,128)}) custom-call(s32[1]{0:T(128)} %bitcast.refs_0_, s32[8]{0:T(128)} %fusion.5.refs_1_, bf16[8,528,2048]{2,1,0:T(8,128)(2,1)} %bitcast.17, bf16[2048,64]{1,0:T(8,128)(2,1)} %copy.20.refs_3_), custom_call_target="tpu_custom_call" | custom-call | flops 12884901888 | bytes 64000000 | tf_op jit(solution)/shard_map/dispatch/pallas_call | solution.py:213
  128.2 79.6 %up.1.refs_0_ = bf16[8,768,1408]{2,1,0:T(8,128)(2,1)} custom-call(bf16[8,768,2048]{2,1,0:T(8,128)(2,1)} %bitcast.18, bf16[8,2048,1408]{2,1,0:T(8,128)(2,1)} %w1_ref.1, bf16[8,2048,1408]{2,1,0:T(8,128)(2,1)} %w3_ref.1), custom_call_target="tpu_custom_call" | custom-call | flops 70866960384 | bytes 100000000 | tf_op jit(solution)/shard_map/up/pallas_call | solution.py:250
  207.9 166.8 %down.1 = bf16[512,2048]{1,0:T(8,128)(2,1)} custom-call(bf16[8,768,1408]{2,1,0:T(8,128)(2,1)} %up.1.refs_0_, bf16[8,1408,2048]{2,1,0:T(8,128)(2,1)} %refs_1_.1, bf16[8,512,768]{2,1,0:T(8,128)(2,1)} %get-tuple-element.9.refs_2_, f32[8,768,128]{2,1,0:T(8,128)} %get-tuple-element.10.refs_3_, f32[512,2048]{1,0:T(8,128)} %ffn.1.refs_4_), custom_call_target="tpu_custom_call" | custom-call | flops 74088185856 | bytes 60000000 | tf_op jit(solution)/shard_map/down/pallas_call | solution.py:456
  374.6 3.2 copy.28
  (3 shorter events, 0.0 us)
Async XLA Ops:
  6.5 94.3 %all-gather.3.cloned.1.call-start = ((), (), s32[]{:S(2)}) async-start(), calls=%async_computation | async-start | bytes 19464192 | tf_op jit(solution)/shard_map/all_gather | solution.py:498
  8.0 1.6 copy-start
Sparse Core Ops, SparseCore 0:
  12.0 88.8 all-gather.2
